TPU v7x, 32 devices: a 4x4x1 block of a 4x4x8 slice. The times are simulated.
32 devices in a mesh: dp: 1 (over z), tp: 4 (over y), ep: 8 (over x, core).
Axes of the slice: x: 4, y: 4, z: 1, core: 2. Of those that a mesh axis runs over, the one named last changes fastest.
The devices are a block of a 4x4x8 slice.
Arguments:
- hidden_in: bfloat16 [1024, 2048], P(('dp', 'ep'))
- positions: int32 [1024], P(('dp', 'ep'))
- expert_ids: int32 [1024, 2], P(('dp', 'ep'))
- k_cache: bfloat16 [1024, 16, 16, 128], P(('dp', 'ep'), None, 'tp')
- v_cache: bfloat16 [1024, 16, 16, 128], P(('dp', 'ep'), None, 'tp')
- norm_in: bfloat16 [2048], replicated
- norm_res: bfloat16 [2048], replicated
- norm_post: bfloat16 [2048], replicated
- w_q: bfloat16 [2048, 2048], P(None, 'tp')
- w_k: bfloat16 [2048, 2048], P(None, 'tp')
- w_v: bfloat16 [2048, 2048], P(None, 'tp')
- w_o: bfloat16 [2048, 2048], P('tp')
- w_gate: bfloat16 [2048, 2816], P(None, 'tp')
- w_up: bfloat16 [2048, 2816], P(None, 'tp')
- w_down: bfloat16 [2816, 2048], P('tp')
- w_router: bfloat16 [2048, 64], replicated
- e_gate: bfloat16 [64, 2048, 1408], P('ep', None, 'tp')
- e_up: bfloat16 [64, 2048, 1408], P('ep', None, 'tp')
- e_down: bfloat16 [64, 1408, 2048], P('ep', 'tp')
Outputs:
- output 1: bfloat16 [1024, 2048], P(('dp', 'ep'))
- output 2: bfloat16 [1024, 16, 16, 128], P(('dp', 'ep'), None, 'tp')
- output 3: bfloat16 [1024, 16, 16, 128], P(('dp', 'ep'), None, 'tp')
All inputs are finite; a program needn't handle non-finite values.
Results may differ from a plain program's by a relative error of at most 0.0135542.
Values are sent between devices in bfloat16 or wider.
A program may use at most 768 MiB of HBM per device.

v0:
```python
import jax
import jax.numpy as jnp
from jax import lax
from jax.sharding import PartitionSpec as P

NORM_EPS = 1e-5
ROPE_BASE = 10000.0


def rms_norm(values, gain_vec):
    wide_vals = values.astype(jnp.float32)
    inv_rms = lax.rsqrt(jnp.mean(wide_vals * wide_vals, axis=-1, keepdims=True) + NORM_EPS)
    return (wide_vals * inv_rms * gain_vec.astype(jnp.float32)).astype(jnp.bfloat16)


def rope_rotate(values, positions):
    half_dim = values.shape[-1] // 2
    inv_freq = 1.0 / (ROPE_BASE ** (jnp.arange(0, 2 * half_dim, 2, dtype=jnp.float32) / (2 * half_dim)))
    angles = positions.astype(jnp.float32)[:, None] * inv_freq[None, :]
    cosine = jnp.cos(angles)[:, None, :]
    sine_part = jnp.sin(angles)[:, None, :]
    first_half = values[..., :half_dim]
    second_half = values[..., half_dim:]
    return jnp.concatenate([first_half * cosine - second_half * sine_part, second_half * cosine + first_half * sine_part], axis=-1)


def attention_block(normed, positions, k_cache, v_cache, w_q, w_k, w_v):
    tokens = normed.shape[0]
    cache_len, kv_heads, head_dim = k_cache.shape[1], k_cache.shape[2], k_cache.shape[3]
    q_heads = w_q.shape[1] // head_dim
    group_size = q_heads // kv_heads
    q_proj = jnp.dot(normed, w_q, preferred_element_type=jnp.float32).reshape(tokens, q_heads, head_dim)
    k_proj = jnp.dot(normed, w_k, preferred_element_type=jnp.float32).reshape(tokens, kv_heads, head_dim)
    v_new = jnp.dot(normed, w_v, preferred_element_type=jnp.float32).astype(jnp.bfloat16).reshape(tokens, kv_heads, head_dim)
    q_rot = rope_rotate(q_proj, positions).astype(jnp.bfloat16).reshape(tokens, kv_heads, group_size, head_dim)
    k_rot = rope_rotate(k_proj, positions).astype(jnp.bfloat16)
    slot_hit = (jnp.arange(cache_len)[None, :] == positions[:, None])[:, :, None, None]
    k_out = jnp.where(slot_hit, k_rot[:, None], k_cache)
    v_out = jnp.where(slot_hit, v_new[:, None], v_cache)
    scores = jnp.einsum('bkgd,btkd->bkgt', q_rot, k_out, preferred_element_type=jnp.float32) * (head_dim ** -0.5)
    visible = jnp.arange(cache_len)[None, None, None, :] <= positions[:, None, None, None]
    attn_probs = jax.nn.softmax(jnp.where(visible, scores, -jnp.inf), axis=-1).astype(jnp.bfloat16)
    mixed_vals = jnp.einsum('bkgt,btkd->bkgd', attn_probs, v_out, preferred_element_type=jnp.float32)
    return mixed_vals.astype(jnp.bfloat16).reshape(tokens, q_heads * head_dim), k_out, v_out


def dense_block(hidden_mid, norm_res, w_gate, w_up, w_down):
    res_in = rms_norm(hidden_mid, norm_res)
    gate_val = jnp.dot(res_in, w_gate, preferred_element_type=jnp.float32)
    up_val = jnp.dot(res_in, w_up, preferred_element_type=jnp.float32)
    act_val = (jax.nn.silu(gate_val) * up_val).astype(jnp.bfloat16)
    return jnp.dot(act_val, w_down, preferred_element_type=jnp.float32)


def route_weights(moe_in, w_router, expert_ids):
    gate_probs = jax.nn.softmax(jnp.dot(moe_in, w_router, preferred_element_type=jnp.float32), axis=-1)
    picked = jnp.take_along_axis(gate_probs, expert_ids, axis=1)
    return picked / jnp.sum(picked, axis=1, keepdims=True)


def run_experts(slot_rows, slot_expert, e_gate, e_up, e_down):
    sort_order = jnp.argsort(slot_expert, stable=True)
    sorted_rows = slot_rows[sort_order]
    group_sizes = jnp.bincount(slot_expert, length=e_gate.shape[0]).astype(jnp.int32)
    gate_val = lax.ragged_dot(sorted_rows, e_gate, group_sizes, preferred_element_type=jnp.float32)
    up_val = lax.ragged_dot(sorted_rows, e_up, group_sizes, preferred_element_type=jnp.float32)
    act_val = (jax.nn.silu(gate_val) * up_val).astype(jnp.bfloat16)
    out_sorted = lax.ragged_dot(act_val, e_down, group_sizes, preferred_element_type=jnp.float32).astype(jnp.bfloat16)
    return out_sorted[jnp.argsort(sort_order)]


def solution(mesh):
    ep_size = mesh.shape['ep']
    row_spec = P(('dp', 'ep'), None)
    cache_spec = P(('dp', 'ep'), None, 'tp', None)
    col_split = P(None, 'tp')
    row_split = P('tp', None)
    in_specs = (row_spec, P(('dp', 'ep')), row_spec, cache_spec, cache_spec, P(None), P(None), P(None), col_split, col_split, col_split, row_split, col_split, col_split, row_split, P(None, None), P('ep', None, 'tp'), P('ep', None, 'tp'), P('ep', 'tp', None))
    out_specs = (row_spec, cache_spec, cache_spec)

    def local_layer(hidden_in, positions, expert_ids, k_cache, v_cache, norm_in, norm_res, norm_post, w_q, w_k, w_v, w_o, w_gate, w_up, w_down, w_router, e_gate, e_up, e_down):
        tokens, model_dim = hidden_in.shape
        local_experts = e_gate.shape[0]
        capacity = 4 * tokens // ep_size
        attn_mix, k_out, v_out = attention_block(rms_norm(hidden_in, norm_in), positions, k_cache, v_cache, w_q, w_k, w_v)
        attn_sum = lax.psum(jnp.dot(attn_mix, w_o, preferred_element_type=jnp.float32).astype(jnp.bfloat16), 'tp')
        hidden_mid = (hidden_in.astype(jnp.float32) + attn_sum.astype(jnp.float32)).astype(jnp.bfloat16)
        dense_sum = lax.psum(dense_block(hidden_mid, norm_res, w_gate, w_up, w_down).astype(jnp.bfloat16), 'tp')
        moe_in = rms_norm(hidden_in, norm_post)
        route_wts = route_weights(moe_in, w_router, expert_ids)
        flat_ids = expert_ids.reshape(-1)
        dest_shard = flat_ids // local_experts
        dest_hot = (dest_shard[:, None] == jnp.arange(ep_size)[None, :]).astype(jnp.int32)
        rank_in_dest = jnp.sum((jnp.cumsum(dest_hot, axis=0) - dest_hot) * dest_hot, axis=1)
        slot_index = dest_shard * capacity + rank_in_dest
        pair_token = jnp.arange(2 * tokens, dtype=jnp.int32) // 2
        send_token = jnp.full((ep_size * capacity,), tokens, jnp.int32).at[slot_index].set(pair_token)
        send_expert = jnp.zeros((ep_size * capacity,), jnp.int32).at[slot_index].set(flat_ids % local_experts)
        padded_rows = jnp.concatenate([moe_in, jnp.zeros((1, model_dim), jnp.bfloat16)], axis=0)
        send_rows = padded_rows[send_token]
        recv_rows = lax.all_to_all(send_rows, 'ep', 0, 0, tiled=True)
        recv_expert = lax.all_to_all(send_expert, 'ep', 0, 0, tiled=True)
        expert_part = run_experts(recv_rows, recv_expert, e_gate, e_up, e_down)
        expert_sum = lax.psum(expert_part, 'tp')
        returned = lax.all_to_all(expert_sum, 'ep', 0, 0, tiled=True)
        pair_out = returned[slot_index].reshape(tokens, 2, model_dim)
        moe_out = jnp.sum(route_wts[:, :, None] * pair_out, axis=1)
        hidden_out = (hidden_mid.astype(jnp.float32) + dense_sum.astype(jnp.float32) + moe_out).astype(jnp.bfloat16)
        return hidden_out, k_out, v_out

    return jax.shard_map(local_layer, mesh=mesh, in_specs=in_specs, out_specs=out_specs, check_vma=False)
```

profile of v0, /device:TPU:96, one launch (start us, length us, event | category | flops | bytes accessed | tf_op | source)
XLA Modules:
  0.0 321.9 jit_solution(4742252782145699760)
XLA Ops:
  7.8 1.2 convert_element_type.93
  9.0 1.3 iota_compare_fusion.1
  10.3 1.2 fusion.16
  12.3 3.0 fusion.59
  15.2 1.7 reshape.343
  17.0 2.8 fusion.57
  19.7 1.7 reshape.344
  21.5 2.7 convolution_convert_fusion.2
  24.2 0.9 broadcast_in_dim.56
  25.2 1.1 multiply_cosine_fusion
  26.3 1.7 subtract_convert_fusion.1
  28.3 6.9 %broadcast_select_fusion = (bf16[128,16,4,128]{3,2,1,0:T(4,128)(2,1)}, bf16[128,16,4,128]{3,2,1,0:T(4,128)(2,1)S(1)}) fusion(bf16[128,16,4,128]{3,2,1,0:T(4,128)(2,1)S(1)} %copy-done.8, pred[128,16]{1,0:T(8,128)(4,1)S(1)} %get-tuple-element.41, bf16[128,4,128]{2,1,0:T(4,128)(2,1)S(1)} %broadcast_in_dim.56, bf16[128,16,4,128]{3,2,1,0:T(4,128)(2,1)} %param.22, ...), kind=kLoop, calls=%fused_computation.17 | loop fusion | flops 2097152 | bytes 8652800 | tf_op jit(solution)/shard_map/jit(_where)/select_n | solution.py:39
  35.3 1.3 copy-done.9
  36.6 1.9 fusion.4
  38.5 1.0 copy.70
  40.6 2.5 fusion.2
  43.2 1.2 convolution_convert_fusion.1
  46.0 1.4 scatter_custom_fusion.1
  48.1 4.0 %all-to-all-start.1 = ((s32[8,64,1]{1,2,0:T(1,128)}), s32[8,64,1]{1,2,0:T(1,128)S(1)}, u32[]{:S(2)}, u32[]{:S(2)}) async-start(s32[8,64,1]{1,2,0:T(1,128)} %bitcast.10), calls=%async_computation.1 | async-start | bytes 8192 | tf_op jit(solution)/shard_map/all_to_all | solution.py:102
  52.1 1.4 scatter_custom_fusion
  53.5 31.5 %all-reduce.5.cloned.1.call-done = bf16[128,2048]{1,0:T(8,128)(2,1)} async-done(((bf16[128,2048]{1,0:T(8,128)(2,1)}), bf16[128,2048]{1,0:T(8,128)(2,1)}) %all-reduce.5.cloned.1.call-update) | async-done | bytes 524304 | tf_op jit(solution)/shard_map/psum | solution.py:86
  85.0 2.1 fusion.18
  88.0 3.3 %gather_fusion = bf16[512,2048]{1,0:T(8,128)(2,1)} fusion(bf16[129,2048]{1,0:T(8,128)(2,1)S(1)} %concatenate.19, s32[1024]{0:T(1024)S(1)} %pad_clamp_fusion.3), kind=kCustom, calls=%fused_computation | custom fusion | bytes 4196352 | tf_op jit(solution)/shard_map/gather | solution.py:100
  91.2 4.5 %all-to-all-start = ((bf16[8,64,2048]{2,1,0:T(8,128)(2,1)}), bf16[8,64,2048]{2,1,0:T(8,128)(2,1)}, u32[]{:S(2)}, u32[]{:S(2)}) async-start(bf16[8,64,2048]{2,1,0:T(8,128)(2,1)} %bitcast.51), calls=%async_computation | async-start | bytes 4194304 | tf_op jit(solution)/shard_map/all_to_all | solution.py:101
  96.0 15.3 %copy.66 = bf16[8,2048,352]{2,1,0:T(8,128)(2,1)} copy(bf16[8,2048,352]{1,2,0:T(8,128)(2,1)} %param.35) | data formatting | bytes 23068672 | tf_op args[16]
  111.3 16.3 %copy.67 = bf16[8,2048,352]{2,1,0:T(8,128)(2,1)} copy(bf16[8,2048,352]{1,2,0:T(8,128)(2,1)} %param.36) | data formatting | bytes 23068672 | tf_op args[17]
  128.9 4.6 %scatter_custom_fusion.2 = s32[8]{0:T(128)} fusion(s32[512]{0:T(512)S(1)} %reshape.408, s32[512]{0:T(512)S(1)} %broadcast.318, s32[]{:T(128)} %constant.89.clone.1), kind=kCustom, calls=%fused_computation.120 | custom fusion | flops 512 | bytes 36 | tf_op jit(solution)/shard_map/scatter-add | solution.py:64
  133.5 1.5 ragged-dot-metadata
  135.0 3.8 %sort.34 = (s32[512]{0:T(512)}, s32[512]{0:T(512)S(1)}) sort(s32[512]{0:T(512)S(1)} %all_to_all.29, s32[512]{0:T(512)S(1)} %iota.42), dimensions={0}, to_apply=%region_14.15 | sort | flops 4608 | bytes 8192 | tf_op jit(solution)/shard_map/jit(argsort)/sort | solution.py:62
  138.8 3.8 %sort.35 = (s32[512]{0:T(512)}, s32[512]{0:T(512)S(1)}) sort(s32[512]{0:T(512)S(1)} %get-tuple-element.5, s32[512]{0:T(512)S(1)} %iota.43), dimensions={0}, to_apply=%region_16.17 | sort | flops 4608 | bytes 8192 | tf_op jit(solution)/shard_map/jit(argsort)/sort | solution.py:69
  142.6 3.6 %fusion.32 = f32[128,704]{0,1:T(8,128)} fusion(bf16[2048,704]{0,1:T(8,128)(2,1)} %param.31, bf16[128,2048]{1,0:T(8,128)(2,1)S(1)} %copy-done.3, f32[2048]{0:T(1024)S(1)} %convert_element_type.101, f32[128]{0:T(128)S(1)} %add_rsqrt_fusion), kind=kOutput, calls=%fused_computation.56 | convolution fusion | flops 370147328 | bytes 3777024 | tf_op jit(solution)/shard_map/dot_general | solution.py:49
  146.2 4.9 %convolution_convert_fusion = bf16[128,2048]{1,0:T(8,128)(2,1)} fusion(bf16[704,2048]{1,0:T(8,128)(2,1)S(1)} %copy-done, bf16[2048,704]{0,1:T(8,128)(2,1)} %param.32, f32[128,704]{0,1:T(8,128)} %fusion.32, bf16[128,2048]{1,0:T(8,128)(2,1)S(1)} %copy-done.3, f32[2048]{0:T(1024)S(1)} %convert_element_type.101, f32[128]{0:T(128)S(1)} %add_rsqrt_fusion), kind=kOutput, calls=%fused_computation.10 | convolution fusion | flops 740048896 | bytes 7184896 | tf_op jit(solution)/shard_map/dot_general | solution.py:52
  151.1 7.1 %gather_fusion.1 = bf16[512,2048]{1,0:T(8,128)(2,1)} fusion(bf16[512,2048]{1,0:T(8,128)(2,1)} %bitcast.12, s32[1024]{0:T(1024)S(1)} %pad_clamp_fusion.2), kind=kCustom, calls=%fused_computation.1 | custom fusion | bytes 4196352 | tf_op jit(solution)/shard_map/gather | solution.py:63
  158.2 14.1 %ragged-dot-none.2 = f32[512,352]{1,0:T(8,128)} custom-call(s32[1]{0:T(128)} %get-tuple-element.7, s32[9]{0:T(128)} %get-tuple-element.8, s32[9]{0:T(128)} %get-tuple-element.9, s32[9]{0:T(128)} %get-tuple-element.10, s32[1]{0:T(128)} %get-tuple-element.7, bf16[512,2048]{1,0:T(8,128)(2,1)} %gather_fusion.1, bf16[8,2048,352]{2,1,0:T(8,128)(2,1)} %copy.66), custom_call_target="tpu_custom_call" | custom-call | flops 738197504 | bytes 14352416 | tf_op jit(solution)/shard_map/ragged_dot_general/ragged-dot-none
  172.3 14.2 %ragged-dot-none.1 = f32[512,352]{1,0:T(8,128)} custom-call(s32[1]{0:T(128)} %get-tuple-element.7, s32[9]{0:T(128)} %get-tuple-element.8, s32[9]{0:T(128)} %get-tuple-element.9, s32[9]{0:T(128)} %get-tuple-element.10, s32[1]{0:T(128)} %get-tuple-element.7, bf16[512,2048]{1,0:T(8,128)(2,1)} %gather_fusion.1, bf16[8,2048,352]{2,1,0:T(8,128)(2,1)} %copy.67), custom_call_target="tpu_custom_call" | custom-call | flops 738197504 | bytes 14352416 | tf_op jit(solution)/shard_map/ragged_dot_general/ragged-dot-none
  186.4 2.1 multiply_convert_fusion
  188.5 14.8 %ragged-dot-none = f32[512,2048]{1,0:T(8,128)} custom-call(s32[1]{0:T(128)} %get-tuple-element.7, s32[9]{0:T(128)} %get-tuple-element.8, s32[9]{0:T(128)} %get-tuple-element.9, s32[9]{0:T(128)} %get-tuple-element.10, s32[1]{0:T(128)} %get-tuple-element.7, bf16[512,352]{1,0:T(8,128)(2,1)} %multiply_convert_fusion, bf16[8,352,2048]{2,1,0:T(8,128)(2,1)} %param.37), custom_call_target="tpu_custom_call" | custom-call | flops 738197504 | bytes 16089120 | tf_op jit(solution)/shard_map/ragged_dot_general/ragged-dot-none
  203.3 2.5 convert_element_type.111
  205.8 3.3 %gather_fusion.2 = bf16[512,2048]{1,0:T(8,128)(2,1)} fusion(bf16[512,2048]{1,0:T(8,128)(2,1)S(1)} %convert_element_type.111, s32[1024]{0:T(1024)S(1)} %pad_clamp_fusion.1), kind=kCustom, calls=%fused_computation.2 | custom fusion | bytes 4196352 | tf_op jit(solution)/shard_map/gather | solution.py:69
  209.2 62.6 %all-reduce.7.cloned.1.call-done = (bf16[8,64,2048]{2,1,0:T(8,128)(2,1)}, bf16[128,2048]{1,0:T(8,128)(2,1)}) async-done(((bf16[8,64,2048]{2,1,0:T(8,128)(2,1)}, bf16[128,2048]{1,0:T(8,128)(2,1)}), (bf16[8,64,2048]{2,1,0:T(8,128)(2,1)}, bf16[128,2048]{1,0:T(8,128)(2,1)})) %all-reduce.7.cloned.1.call-update) | async-done | bytes 2621456 | tf_op jit(solution)/shard_map/psum | solution.py:104
  271.8 4.4 %all-to-all-start.2 = ((bf16[8,64,2048]{2,1,0:T(8,128)(2,1)}), bf16[8,64,2048]{2,1,0:T(8,128)(2,1)S(1)}, u32[]{:S(2)}, u32[]{:S(2)}) async-start(bf16[8,64,2048]{2,1,0:T(8,128)(2,1)} %get-tuple-element.21), calls=%async_computation.2 | async-start | bytes 4194304 | tf_op jit(solution)/shard_map/all_to_all | solution.py:105
  276.5 1.3 fusion.64
  277.8 2.0 gather_fusion.4
  280.1 23.2 %all-to-all-done.2 = bf16[8,64,2048]{2,1,0:T(8,128)(2,1)S(1)} async-done(((bf16[8,64,2048]{2,1,0:T(8,128)(2,1)}), bf16[8,64,2048]{2,1,0:T(8,128)(2,1)S(1)}, u32[]{:S(2)}, u32[]{:S(2)}) %all-to-all-start.2) | async-done | bytes 2097184 | tf_op jit(solution)/shard_map/all_to_all | solution.py:105
  303.4 2.3 gather_fusion.3
  305.7 3.4 %reshape.351 = f32[128,2,2048]{2,1,0:T(2,128)} reshape(bf16[256,2048]{1,0:T(8,128)(2,1)} %gather_fusion.3) | data formatting | bytes 3145728 | tf_op jit(solution)/shard_map/convert_element_type | solution.py:107
  309.1 5.0 %multiply_reduce_fusion = f32[128,2048]{1,0:T(8,128)S(1)} fusion(f32[128,2,2048]{2,1,0:T(2,128)} %reshape.351, f32[128,2]{1,0:T(8,128)S(1)} %copy.61), kind=kLoop, calls=%fused_computation.16 | loop fusion | flops 786432 | bytes 3146752 | tf_op jit(solution)/shard_map/reduce_sum | solution.py:107
  314.1 1.0 fusion.22
  (91 shorter events, 8.2 us)
Async XLA Ops:
  7.2 139.0 %copy-start = (bf16[704,2048]{1,0:T(8,128)(2,1)S(1)}, bf16[704,2048]{1,0:T(8,128)(2,1)}, u32[]{:S(2)}) copy-start(bf16[704,2048]{1,0:T(8,128)(2,1)} %param.33) | copy-start | bytes 8650756
  7.2 9.8 %copy-start.2 = (bf16[128,2048]{1,0:T(8,128)(2,1)S(1)}, bf16[128,2048]{1,0:T(8,128)(2,1)}, u32[]{:S(2)}) copy-start(bf16[128,2048]{1,0:T(8,128)(2,1)} %param.19) | copy-start | bytes 1572868
  7.2 77.8 %all-reduce.5.cloned.1.call-start = ((), (), s32[]{:S(2)}) async-start(), calls=%async_computation.3 | async-start | bytes 1048576 | tf_op jit(solution)/shard_map/psum | solution.py:86
  11.6 9.9 %copy-start.13 = (f32[128]{0:T(128)}, f32[128]{0:T(128)S(1)}, u32[]{:S(2)}) copy-start(f32[128]{0:T(128)S(1)} %add_rsqrt_fusion.1) | copy-start | bytes 1540
  25.2 3.2 copy-start.8
  35.3 1.3 copy-start.9
  35.3 4.2 %copy-start.11 = (pred[128,16]{1,0:T(8,128)(4,1)S(1)}, pred[128,16]{1,0:T(8,128)(4,1)}, u32[]{:S(2)}) copy-start(pred[128,16]{1,0:T(8,128)(4,1)} %get-tuple-element.40) | copy-start | bytes 6148
  40.6 2.6 copy-start.7
  43.1 1.4 copy-start.12
  43.1 9.0 %copy-start.15 = (bf16[2048]{0:T(1024)(128)(2,1)S(1)}, bf16[2048]{0:T(1024)(128)(2,1)}, u32[]{:S(2)}) copy-start(bf16[2048]{0:T(1024)(128)(2,1)} %param.26) | copy-start | bytes 12292
  43.1 41.9 %copy-start.14 = (f32[128]{0:T(128)S(1)}, f32[128]{0:T(128)}, u32[]{:S(2)}) copy-start(f32[128]{0:T(128)} %copy-done.13) | copy-start | bytes 1540
  48.1 43.1 %all-to-all-start.1 = ((s32[8,64,1]{1,2,0:T(1,128)}), s32[8,64,1]{1,2,0:T(1,128)S(1)}, u32[]{:S(2)}, u32[]{:S(2)}) async-start(s32[8,64,1]{1,2,0:T(1,128)} %bitcast.10), calls=%async_computation.1 | async-start | bytes 8192 | tf_op jit(solution)/shard_map/all_to_all | solution.py:102
  87.1 0.8 copy-start.4
  91.2 59.8 %all-to-all-start = ((bf16[8,64,2048]{2,1,0:T(8,128)(2,1)}), bf16[8,64,2048]{2,1,0:T(8,128)(2,1)}, u32[]{:S(2)}, u32[]{:S(2)}) async-start(bf16[8,64,2048]{2,1,0:T(8,128)(2,1)} %bitcast.51), calls=%async_computation | async-start | bytes 4194304 | tf_op jit(solution)/shard_map/all_to_all | solution.py:101
  95.8 176.0 %all-reduce.7.cloned.1.call-start = ((), (), s32[]{:S(2)}) async-start(), calls=%async_computation.4 | async-start | bytes 5242880 | tf_op jit(solution)/shard_map/psum | solution.py:104
  111.3 16.3 %copy-start.16 = (bf16[2048]{0:T(1024)(128)(2,1)S(1)}, bf16[2048]{0:T(1024)(128)(2,1)}, u32[]{:S(2)}) copy-start(bf16[2048]{0:T(1024)(128)(2,1)} %param.25) | copy-start | bytes 12292
  111.3 31.3 %copy-start.3 = (bf16[128,2048]{1,0:T(8,128)(2,1)S(1)}, bf16[128,2048]{1,0:T(8,128)(2,1)}, u32[]{:S(2)}) copy-start(bf16[128,2048]{1,0:T(8,128)(2,1)} %get-tuple-element.26) | copy-start | bytes 1572868
  172.2 14.2 %copy-start.6 = (f32[512,352]{1,0:T(8,128)S(1)}, f32[512,352]{1,0:T(8,128)}, u32[]{:S(2)}) copy-start(f32[512,352]{1,0:T(8,128)} %ragged-dot-none.2) | copy-start | bytes 2162692
  271.8 4.7 %copy-start.5 = (bf16[128,2048]{1,0:T(8,128)(2,1)S(1)}, bf16[128,2048]{1,0:T(8,128)(2,1)}, u32[]{:S(2)}) copy-start(bf16[128,2048]{1,0:T(8,128)(2,1)} %copy-done.4) | copy-start | bytes 1572868
  271.8 31.6 %all-to-all-start.2 = ((bf16[8,64,2048]{2,1,0:T(8,128)(2,1)}), bf16[8,64,2048]{2,1,0:T(8,128)(2,1)S(1)}, u32[]{:S(2)}, u32[]{:S(2)}) async-start(bf16[8,64,2048]{2,1,0:T(8,128)(2,1)} %get-tuple-element.21), calls=%async_computation.2 | async-start | bytes 4194304 | tf_op jit(solution)/shard_map/all_to_all | solution.py:105
  309.1 5.0 %copy-start.10 = (bf16[128,2048]{1,0:T(8,128)(2,1)S(1)}, bf16[128,2048]{1,0:T(8,128)(2,1)}, u32[]{:S(2)}) copy-start(bf16[128,2048]{1,0:T(8,128)(2,1)} %get-tuple-element.22) | copy-start | bytes 1572868
  309.1 6.0 %copy-start.1 = (bf16[704,2048]{1,0:T(8,128)(2,1)S(1)}, bf16[704,2048]{1,0:T(8,128)(2,1)}, u32[]{:S(2)}) copy-start(bf16[704,2048]{1,0:T(8,128)(2,1)} %param.33) | copy-start | bytes 8650756
Sparse Core Ops, SparseCore 0:
  44.6 40.3 all-reduce.4
  209.3 62.4 all-reduce.6
where the time goes:
time: 325 us; the launch traced here: 322 us
  waiting for transfers between devices  117 us (36%)
  local copies, waits for them, and re-layouts  67 us (21%)
  Pallas kernels  44.5 us (14%)
  other arithmetic  41.4 us (13%)
  matrix products  23.9 us (7%)
  between operations  14.5 us (4%)
  starting transfers between devices  13.2 us (4%)
    psum x1, waiting for transfers between devices, local_layer(): expert_sum = lax.psum(expert_part, 'tp')  62.6 us
    another operation x3, Pallas kernels  43 us
    unnamed x37, local copies, waits for them, and re-layouts  33.9 us
    psum x1, waiting for transfers between devices, local_layer(): lax.psum(jnp.dot(attn_mix, w_o, preferred_element_type=jnp.float32).astyp...  31.5 us
    all_to_all x1, waiting for transfers between devices, local_layer(): returned = lax.all_to_all(expert_sum, 'ep', 0, 0, tiled=True)  23.2 us
    gather x1, local copies, waits for them, and re-layouts, run_experts(): sorted_rows = slot_rows[sort_order]  7.08 us
    select_n x1, other arithmetic, attention_block(): v_out = jnp.where(slot_hit, v_new[:, None], v_cache)  6.92 us
  transfers between devices with their start and end apart: 5, of which 3 were waited for; matrix products, arithmetic and copies ran while one was open for 21% of the time, Pallas kernels for 0%

commit v1 on v0

v1 whole, which is shorter than its diff:
```python
import functools

import jax
import jax.numpy as jnp
import numpy as np
from jax import lax
from jax.experimental import pallas as pl
from jax.experimental.pallas import tpu as pltpu
from jax.sharding import PartitionSpec as P

NORM_EPS = 1e-5
ROPE_BASE = 10000.0
F32 = jnp.float32
BF16 = jnp.bfloat16
MESH = pl.DeviceIdType.MESH
ROWS = 256
ALIGN = 16


def rms_norm(values, gain_row):
    wide_vals = values.astype(F32)
    inv_rms = lax.rsqrt(jnp.mean(wide_vals * wide_vals, axis=-1, keepdims=True) + NORM_EPS)
    return (wide_vals * inv_rms * gain_row.astype(F32)).astype(BF16)


def dot_nn(a, b):
    return lax.dot_general(a, b, (((1,), (0,)), ((), ())), preferred_element_type=F32)


def dot_nt(a, b):
    return lax.dot_general(a, b, (((1,), (1,)), ((), ())), preferred_element_type=F32)


def lane_scan(values):
    lane = lax.broadcasted_iota(jnp.int32, values.shape, 1)
    step = 1
    while step < values.shape[1]:
        values = values + jnp.where(lane >= step, pltpu.roll(values, step, 1), 0)
        step *= 2
    return values


def row_scan(values):
    row = lax.broadcasted_iota(jnp.int32, values.shape, 0)
    step = 1
    while step < values.shape[0]:
        values = values + jnp.where(row >= step, pltpu.roll(values, step, 0), 0)
        step *= 2
    return values


def layer_kernel(
    n_tp, n_ep, ep_axis, tp_axis,
    x_ref, pos_row_ref, pos_smem, ids_ref, n_in_ref, n_res_ref, n_post_ref, w_router_ref, rope_ref,
    k_hbm, v_hbm, wq_hbm, wk_hbm, wv_hbm, wo_hbm, wg_hbm, wu_hbm, wd_hbm, eg_hbm, eu_hbm, ed_hbm,
    out_ref, k_out, v_out,
    eg, eu, ed, rows_all, meta, all_ids, part_q, part_in, h_q, c_buf, d_in, r1_in, r2_in, dense_q, fin_q, fin_in, out_q,
    sched_v, sched,
    w_sem, e_sem, ag_send, ag_recv, m_send, m_recv, i_send, i_recv, a_send, a_recv, h_send, h_recv, d_send, d_recv,
    r1_send, r1_recv, r2_send, r2_recv, f_send, f_recv, o_send, o_recv,
):
    tokens, dim = x_ref.shape
    quarter = dim // n_tp
    n_x = n_ep // 2
    half = tokens // 2
    n_local, width = eg.shape[0], eg.shape[1]
    cache_len, heads, head_dim = k_hbm.shape[1], k_hbm.shape[2], k_hbm.shape[3]
    n_blocks = n_ep
    all_rows = n_blocks * tokens
    n_sorted = -(-(4 * tokens + n_local * (ALIGN - 1)) // 128) * 128
    n_steps = n_local + 1
    dense_parts = wd_hbm.shape[0]

    ep = lax.axis_index(ep_axis)
    tp = lax.axis_index(tp_axis)
    chip = ep // 2
    core = ep % 2
    other = 1 - core
    right = (chip + 1) % n_x
    left = (chip + n_x - 1) % n_x
    far = (chip + 2) % n_x

    def on_ring(place):
        return {ep_axis: place * 2 + core}

    partner = {ep_axis: chip * 2 + other}

    def ep_peer(k):
        return {ep_axis: (ep + k) % n_ep}

    def tp_peer(k):
        return {tp_axis: (tp + k) % n_tp}

    def remote(src, dst, send_sem, recv_sem, device):
        return pltpu.make_async_remote_copy(
            src_ref=src, dst_ref=dst, send_sem=send_sem, recv_sem=recv_sem, device_id=device, device_id_type=MESH)

    def arrived(dst, recv_sem):
        remote(dst, dst, recv_sem, recv_sem, partner).wait_recv()

    def sent(src, send_sem):
        remote(src, src, send_sem, send_sem, partner).wait_send()

    low, high = pl.ds(0, half), pl.ds(half, half)

    def forward(index, place, rows):
        block = rows_all.at[core, place, rows]
        arrived(block, ag_recv.at[index])
        remote(block, block, ag_send.at[index + 6], ag_recv.at[index + 6], partner).start()

    def forward_first():
        forward(1, left, low)
        block = rows_all.at[core, left, low]
        remote(block, block, ag_send.at[5], ag_recv.at[5], on_ring(right)).start()
        forward(3, right, high)
        block = rows_all.at[core, right, high]
        remote(block, block, ag_send.at[6], ag_recv.at[6], on_ring(left)).start()

    barrier = pltpu.get_barrier_semaphore()
    for k in range(1, n_ep):
        pl.semaphore_signal(barrier, inc=1, device_id=ep_peer(k), device_id_type=MESH)
    for k in range(1, n_tp):
        pl.semaphore_signal(barrier, inc=1, device_id=tp_peer(k), device_id_type=MESH)

    def attention_phase(wq, wk, wv, wo, kc, vc, q_s, k_s, v_s, o_s):
        loads = [
            pltpu.make_async_copy(src, dst, w_sem.at[i])
            for i, (src, dst) in enumerate(
                ((wq_hbm, wq), (wk_hbm, wk), (wv_hbm, wv), (k_hbm, kc), (v_hbm, vc), (wo_hbm, wo)))
        ]
        for load in loads:
            load.start()

        moe_in = rms_norm(x_ref[...], n_post_ref[...])
        rows_all[core, chip] = moe_in
        logits = dot_nt(w_router_ref[...], moe_in)
        shifted = jnp.exp(logits - jnp.max(logits, axis=0, keepdims=True))
        probs = shifted / jnp.sum(shifted, axis=0, keepdims=True)
        expert_row = lax.broadcasted_iota(jnp.int32, probs.shape, 0)
        ids = ids_ref[...]
        picked = [
            jnp.sum(jnp.where(expert_row == ids[k:k + 1, :], probs, 0.0), axis=0, keepdims=True) for k in range(2)
        ]
        total = picked[0] + picked[1]
        meta[core * n_x + chip] = jnp.concatenate(
            [picked[0] / total, picked[1] / total, jnp.zeros((6, tokens), F32)], axis=0)
        all_ids[core * n_x + chip] = jnp.concatenate([ids, jnp.zeros((6, tokens), jnp.int32)], axis=0)

        pl.semaphore_wait(barrier, n_ep - 1 + n_tp - 1)
        own = rows_all.at[core, chip]
        sends = [
            remote(own.at[low], own.at[low], ag_send.at[1], ag_recv.at[1], on_ring(right)),
            remote(own.at[high], own.at[high], ag_send.at[3], ag_recv.at[3], on_ring(left)),
            remote(own.at[high], own.at[high], ag_send.at[2], ag_recv.at[2], on_ring(right)),
            remote(own.at[low], own.at[low], ag_send.at[4], ag_recv.at[4], on_ring(left)),
            remote(own, own, ag_send.at[0], ag_recv.at[0], partner),
        ]
        for k in range(1, n_ep):
            block = meta.at[core * n_x + chip]
            sends.append(remote(block, block, m_send.at[k - 1], m_recv.at[k - 1], ep_peer(k)))
            block = all_ids.at[core * n_x + chip]
            sends.append(remote(block, block, i_send.at[k - 1], i_recv.at[k - 1], ep_peer(k)))
        for send in sends:
            send.start()

        normed = rms_norm(x_ref[...], n_in_ref[...])
        pos_col = jnp.transpose(jnp.broadcast_to(pos_row_ref[...].astype(F32), (tokens, tokens)))
        cosine = jnp.zeros((tokens, head_dim), F32)
        sine = jnp.zeros((tokens, head_dim), F32)
        for p in range(cache_len):
            cosine = jnp.where(pos_col == float(p), rope_ref[p:p + 1, :], cosine)
            sine = jnp.where(pos_col == float(p), rope_ref[cache_len + p:cache_len + p + 1, :], sine)

        def rotated(values):
            return values * cosine + pltpu.roll(values, head_dim // 2, 1) * sine

        for load, weights, dest, turn in (
            (loads[0], wq, q_s, True), (loads[1], wk, k_s, True), (loads[2], wv, v_s, False)):
            load.wait()
            proj = dot_nn(normed, weights[...])
            for head in range(heads):
                values = proj[:, head * head_dim:(head + 1) * head_dim]
                values = rotated(values) if turn else values
                dest[:, head, :] = values.astype(BF16).astype(F32)

        for e in range(n_local):
            pltpu.make_async_copy(eg_hbm.at[e], eg.at[e], e_sem.at[0, e]).start()
            pltpu.make_async_copy(eu_hbm.at[e], eu.at[e], e_sem.at[1, e]).start()
            pltpu.make_async_copy(ed_hbm.at[e], ed.at[e], e_sem.at[2, e]).start()

        loads[3].wait()
        loads[4].wait()
        slot = lax.broadcasted_iota(jnp.int32, (cache_len, heads, head_dim), 0)
        slot_one = lax.broadcasted_iota(jnp.int32, (cache_len, heads, 1), 0)
        unroll = 4

        def attend(group, carry):
            for i in range(unroll):
                t = group * unroll + i
                at = pos_smem[t]
                keys = jnp.where(slot == at, k_s[t][None], kc[t].astype(F32))
                kc[t] = keys.astype(BF16)
                scores = jnp.sum(keys * q_s[t][None], axis=-1, keepdims=True) * (head_dim ** -0.5)
                scores = jnp.where(slot_one <= at, scores, -jnp.inf)
                weights = jnp.exp(scores - jnp.max(scores, axis=0, keepdims=True))
                weights = weights / jnp.sum(weights, axis=0, keepdims=True)
                weights = weights.astype(BF16).astype(F32)
                vals = jnp.where(slot == at, v_s[t][None], vc[t].astype(F32))
                vc[t] = vals.astype(BF16)
                visible_vals = jnp.where(slot <= at, vals, 0.0)
                o_s[t] = jnp.sum(weights * visible_vals, axis=0)
            return carry

        lax.fori_loop(0, tokens // unroll, attend, 0)
        stores = [pltpu.make_async_copy(kc, k_out, w_sem.at[6]), pltpu.make_async_copy(vc, v_out, w_sem.at[7])]
        for store in stores:
            store.start()

        forward_first()

        mixed = jnp.concatenate([o_s[:, head, :] for head in range(heads)], axis=1).astype(BF16)
        loads[5].wait()
        for q in range(n_tp):
            part_q[q] = dot_nn(mixed, wo[:, q * quarter:(q + 1) * quarter]).astype(BF16)
        for k in range(1, n_tp):
            send = remote(part_q.at[(tp + k) % n_tp], part_in.at[k - 1], a_send.at[k - 1], a_recv.at[k - 1], tp_peer(k))
            send.start()
        for store in stores:
            store.wait()

    pl.run_scoped(
        attention_phase,
        *[pltpu.VMEM((dim, heads * head_dim), BF16)] * 3,
        pltpu.VMEM((heads * head_dim, dim), BF16),
        *[pltpu.VMEM((tokens, cache_len, heads, head_dim), BF16)] * 2,
        *[pltpu.VMEM((tokens, heads, head_dim), F32)] * 4,
    )

    forward(2, left, high)
    forward(4, right, low)

    mine = pl.ds(pl.multiple_of(tp * quarter, quarter), quarter)
    for k in range(1, n_tp):
        arrived(part_in.at[k - 1], a_recv.at[k - 1])
    attn_sum = part_q[tp].astype(F32)
    for k in range(1, n_tp):
        attn_sum = attn_sum + part_in[k - 1].astype(F32)
    h_q[tp] = (x_ref[:, mine].astype(F32) + attn_sum).astype(BF16)
    for k in range(1, n_tp):
        remote(h_q.at[tp], h_q.at[tp], h_send.at[k - 1], h_recv.at[k - 1], tp_peer(k)).start()

    forward(5, far, low)
    forward(6, far, high)

    def expert_phase(xs, sort, unsort, z, ys, y_sorted, weight_sorted):
        for k in range(1, n_ep):
            source = (ep + n_ep - k) % n_ep
            arrived(meta.at[(source % 2) * n_x + source // 2], m_recv.at[k - 1])
            arrived(all_ids.at[(source % 2) * n_x + source // 2], i_recv.at[k - 1])
        ids = [all_ids[:, k, :] for k in range(2)]
        wts = [meta[:, k, :] for k in range(2)]
        first = ep * n_local
        lane = lax.broadcasted_iota(jnp.int32, (n_blocks, tokens), 1)
        start = jnp.zeros((n_blocks, tokens), jnp.int32)
        place = jnp.full((n_blocks, tokens), -1, jnp.int32)
        weight = jnp.zeros((n_blocks, tokens), F32)
        step_expert = jnp.zeros((n_blocks, tokens), jnp.int32)
        step_row = jnp.zeros((n_blocks, tokens), jnp.int32)
        block_row = jnp.zeros((n_blocks, tokens), jnp.int32)
        for e in range(n_local):
            here = [i == first + e for i in ids]
            hit = jnp.where(jnp.logical_or(here[0], here[1]), 1, 0)
            weight = jnp.where(here[0], wts[0], jnp.where(here[1], wts[1], weight))
            scan = lane_scan(hit)
            totals = jnp.broadcast_to(scan[:, tokens - 1:], scan.shape)
            above = row_scan(totals)
            count = jnp.broadcast_to(above[n_blocks - 1:, :], scan.shape)
            place = jnp.where(hit == 1, start + above - totals + scan - 1, place)
            step_row = jnp.where(lane == e, start, step_row)
            step_expert = jnp.where(lane == e, e, step_expert)
            spill = jnp.logical_and(lane == n_local, count > ROWS)
            step_row = jnp.where(spill, start + ROWS, step_row)
            step_expert = jnp.where(spill, e, step_expert)
            later = start + (count + ALIGN - 1) // ALIGN * ALIGN
            into = lane * ALIGN - start
            inside = jnp.logical_and(into >= 0, lane * ALIGN < later)
            block_row = jnp.where(
                inside, jnp.where(into < ROWS, e * ROWS + into, n_local * ROWS + into - ROWS), block_row)
            start = later
        step_row = jnp.minimum(step_row, n_sorted)
        block_row = jnp.minimum(block_row, n_steps * ROWS - ALIGN)
        table_row = lax.broadcasted_iota(jnp.int32, (n_blocks, tokens), 0)
        sched_v[...] = jnp.where(
            table_row == 0, step_expert, jnp.where(table_row == 1, step_row // ALIGN, block_row // ALIGN))
        to_scalar = pltpu.make_async_copy(sched_v, sched, w_sem.at[8])
        to_scalar.start()

        row_id = lax.broadcasted_iota(jnp.int32, (n_sorted, tokens), 0)
        weight_rows = jnp.zeros((n_sorted, tokens), F32)
        for j in range(n_blocks):
            match = row_id == place[j:j + 1, :]
            sort[:, j * tokens:(j + 1) * tokens] = jnp.where(match, 1.0, 0.0).astype(BF16)
            weight_rows = weight_rows + jnp.where(match, weight[j:j + 1, :], 0.0)
        weight_sorted[0:n_sorted, :] = jnp.broadcast_to(
            jnp.sum(weight_rows, axis=1, keepdims=True), (n_sorted, 128))
        weight_sorted[n_sorted:, :] = jnp.zeros((ROWS, 128), F32)
        xs[n_sorted:, :] = jnp.zeros((ROWS, dim), BF16)
        place_cols = jnp.transpose(place.astype(F32))
        column_id = lax.broadcasted_iota(jnp.int32, (tokens, n_sorted), 1).astype(F32)
        for j in range(n_blocks):
            unsort[j * tokens:(j + 1) * tokens, :] = jnp.where(
                column_id == place_cols[:, j:j + 1], 1.0, 0.0).astype(BF16)

        arrived(rows_all.at[other, chip], ag_recv.at[0])
        for index, spot, part in ((1, left, low), (2, left, high), (3, right, high), (4, right, low), (5, far, low), (6, far, high)):
            arrived(rows_all.at[other, spot, part], ag_recv.at[index + 6])
        for index in range(1, 13):
            sent(rows_all.at[core, chip, low], ag_send.at[index])
        sent(rows_all.at[core, chip], ag_send.at[0])
        for k in range(1, n_ep):
            sent(meta.at[core * n_x + chip], m_send.at[k - 1])
            sent(all_ids.at[core * n_x + chip], i_send.at[k - 1])

        def sort_columns(i, carry):
            cols = pl.ds(pl.multiple_of(i * 256, 256), 256)
            rows = rows_all[:, :, :, cols].reshape(all_rows, 256)
            xs[0:n_sorted, cols] = dot_nn(sort[...], rows).astype(BF16)
            return carry

        lax.fori_loop(0, dim // 256, sort_columns, 0)
        to_scalar.wait()
        for e in range(n_local):
            pltpu.make_async_copy(eg_hbm.at[e], eg.at[e], e_sem.at[0, e]).wait()
            pltpu.make_async_copy(eu_hbm.at[e], eu.at[e], e_sem.at[1, e]).wait()

        def gate_up(step, carry):
            e = sched[0, step]
            rows = xs[pl.ds(sched[1, step] * ALIGN, ROWS), :]
            act = jax.nn.silu(dot_nt(eg[e], rows)) * dot_nt(eu[e], rows)
            z[step] = jnp.transpose(act).astype(BF16)
            return carry

        lax.fori_loop(0, n_steps, gate_up, 0)

        for p in range(dense_parts):
            pltpu.make_async_copy(wg_hbm.at[p], eg.at[p], w_sem.at[p]).start()
            pltpu.make_async_copy(wu_hbm.at[p], eu.at[p], w_sem.at[2 + p]).start()
            pltpu.make_async_copy(wd_hbm.at[p], eg.at[dense_parts + p], w_sem.at[4 + p]).start()
        for e in range(n_local):
            pltpu.make_async_copy(ed_hbm.at[e], ed.at[e], e_sem.at[2, e]).wait()

        for i in range(n_tp):
            cols = columns(i)

            def down(step, carry):
                e = sched[0, step]
                scale = weight_sorted[pl.ds(sched[1, step] * ALIGN, ROWS), :]
                prod = dot_nn(z[step], ed[e, :, cols])
                scaled = [prod[:, b * 128:(b + 1) * 128] * scale for b in range(quarter // 128)]
                ys[pl.ds(pl.multiple_of(step * ROWS, ROWS), ROWS), :] = jnp.concatenate(scaled, axis=1).astype(BF16)
                return carry

            lax.fori_loop(0, n_steps, down, 0)

            def regroup(b, carry):
                y_sorted[pl.ds(pl.multiple_of(b * ALIGN, ALIGN), ALIGN), :] = ys[
                    pl.ds(sched[2, b] * ALIGN, ALIGN), :]
                return carry

            lax.fori_loop(0, n_sorted // ALIGN, regroup, 0)
            for c in range(2):
                back = dot_nn(unsort[c * n_x * tokens:(c + 1) * n_x * tokens, :], y_sorted[...])
                rows_all[c, :, :, cols] = back.astype(BF16).reshape(n_x, tokens, quarter)
            remote(rows_all.at[other, :, :, cols], d_in.at[i], d_send.at[i], d_recv.at[i], partner).start()
            if i >= 1:
                pair_sum(i - 1)
            if i >= 2:
                ring_sum(i - 2)

    def columns(i):
        return pl.ds(pl.multiple_of(((tp + 1 + i) % n_tp) * quarter, quarter), quarter)

    def pair_sum(i):
        cols = columns(i)
        arrived(d_in.at[i], d_recv.at[i])
        for spot in range(n_x):
            rows_all[core, spot, :, cols] = (
                rows_all[core, spot, :, cols].astype(F32) + d_in[i, spot].astype(F32)).astype(BF16)
        remote(rows_all.at[core, far, low, cols], r1_in.at[i, 0], r1_send.at[i, 0], r1_recv.at[i, 0], on_ring(right)).start()
        remote(rows_all.at[core, far, high, cols], r1_in.at[i, 1], r1_send.at[i, 1], r1_recv.at[i, 1], on_ring(left)).start()
        remote(rows_all.at[core, right, high, cols], r2_in.at[i, 0, high], r2_send.at[i, 0], r2_recv.at[i, 0], on_ring(right)).start()
        remote(rows_all.at[core, left, low, cols], r2_in.at[i, 1, low], r2_send.at[i, 1], r2_recv.at[i, 1], on_ring(left)).start()

    def ring_sum(i):
        cols = columns(i)
        arrived(r1_in.at[i, 0], r1_recv.at[i, 0])
        rows_all[core, right, low, cols] = (
            rows_all[core, right, low, cols].astype(F32) + r1_in[i, 0].astype(F32)).astype(BF16)
        remote(rows_all.at[core, right, low, cols], r2_in.at[i, 0, low], r2_send.at[i, 2], r2_recv.at[i, 2], on_ring(right)).start()
        arrived(r1_in.at[i, 1], r1_recv.at[i, 1])
        rows_all[core, left, high, cols] = (
            rows_all[core, left, high, cols].astype(F32) + r1_in[i, 1].astype(F32)).astype(BF16)
        remote(rows_all.at[core, left, high, cols], r2_in.at[i, 1, high], r2_send.at[i, 3], r2_recv.at[i, 3], on_ring(left)).start()

    pl.run_scoped(
        expert_phase,
        pltpu.VMEM((n_sorted + ROWS, dim), BF16),
        pltpu.VMEM((n_sorted, all_rows), BF16),
        pltpu.VMEM((all_rows, n_sorted), BF16),
        pltpu.VMEM((n_steps, ROWS, width), BF16),
        pltpu.VMEM((n_steps * ROWS, quarter), BF16),
        pltpu.VMEM((n_sorted, quarter), BF16),
        pltpu.VMEM((n_sorted + ROWS, 128), F32),
    )
    pair_sum(n_tp - 1)
    ring_sum(n_tp - 2)

    for k in range(1, n_tp):
        source = (tp + n_tp - k) % n_tp
        arrived(h_q.at[source], h_recv.at[k - 1])
    hidden_mid = jnp.concatenate([h_q[q] for q in range(n_tp)], axis=1)
    c_buf[...] = rms_norm(hidden_mid, n_res_ref[...])
    acts = []
    for p in range(dense_parts):
        pltpu.make_async_copy(wg_hbm.at[p], eg.at[p], w_sem.at[p]).wait()
        pltpu.make_async_copy(wu_hbm.at[p], eu.at[p], w_sem.at[2 + p]).wait()
        act = jax.nn.silu(dot_nt(eg[p], c_buf[...])) * dot_nt(eu[p], c_buf[...])
        acts.append(jnp.transpose(act).astype(BF16))
    for p in range(dense_parts):
        pltpu.make_async_copy(wd_hbm.at[p], eg.at[dense_parts + p], w_sem.at[4 + p]).wait()
    for q in range(n_tp):
        cols = slice(q * quarter, (q + 1) * quarter)
        dense = dot_nn(acts[0], eg[dense_parts, :, cols])
        for p in range(1, dense_parts):
            dense = dense + dot_nn(acts[p], eg[dense_parts + p, :, cols])
        dense_q[q] = dense
    ring_sum(n_tp - 1)

    for i in range(n_tp):
        q = (tp + 1 + i) % n_tp
        cols = columns(i)
        arrived(r2_in.at[i, 0, high], r2_recv.at[i, 0])
        arrived(r2_in.at[i, 1, low], r2_recv.at[i, 1])
        arrived(r2_in.at[i, 0, low], r2_recv.at[i, 2])
        arrived(r2_in.at[i, 1, high], r2_recv.at[i, 3])
        part = rows_all[core, chip, :, cols].astype(F32) + r2_in[i, 0].astype(F32) + r2_in[i, 1].astype(F32) + dense_q[q]
        if i < n_tp - 1:
            fin_q[i] = part.astype(BF16)
            remote(fin_q.at[i], fin_in.at[i], f_send.at[i], f_recv.at[i], tp_peer(i + 1)).start()
        else:
            for k in range(1, n_tp):
                arrived(fin_in.at[k - 1], f_recv.at[k - 1])
                part = part + fin_in[k - 1].astype(F32)
            out_q[tp] = (h_q[tp].astype(F32) + part).astype(BF16)
    for k in range(1, n_tp):
        remote(out_q.at[tp], out_q.at[tp], o_send.at[k - 1], o_recv.at[k - 1], tp_peer(k)).start()

    for i in range(n_tp):
        cols = columns(i)
        sent(d_in.at[i], d_send.at[i])
        for side in range(2):
            sent(r1_in.at[i, side], r1_send.at[i, side])
        for message in range(4):
            sent(r1_in.at[i, 0], r2_send.at[i, message])
    for k in range(1, n_tp):
        sent(part_in.at[k - 1], a_send.at[k - 1])
        sent(part_in.at[k - 1], h_send.at[k - 1])
        sent(part_in.at[k - 1], f_send.at[k - 1])
    for k in range(1, n_tp):
        source = (tp + n_tp - k) % n_tp
        arrived(out_q.at[source], o_recv.at[k - 1])
    for q in range(n_tp):
        out_ref[:, q * quarter:(q + 1) * quarter] = out_q[q]
    for k in range(1, n_tp):
        sent(part_in.at[k - 1], o_send.at[k - 1])


def rope_table(cache_len, head_dim):
    freq = 1.0 / (ROPE_BASE ** (np.arange(0, head_dim, 2, dtype=np.float32) / np.float32(head_dim)))
    angle = np.arange(cache_len, dtype=np.float32)[:, None] * freq.astype(np.float32)[None, :]
    cosine, sine = np.cos(angle), np.sin(angle)
    return np.concatenate(
        [np.concatenate([cosine, cosine], 1), np.concatenate([-sine, sine], 1)], 0).astype(np.float32)


def solution(mesh):
    n_tp, n_ep = mesh.shape['tp'], mesh.shape['ep']
    row_spec = P(('dp', 'ep'), None)
    cache_spec = P(('dp', 'ep'), None, 'tp', None)
    col_split = P(None, 'tp')
    row_split = P('tp', None)
    in_specs = (row_spec, P(('dp', 'ep')), row_spec, cache_spec, cache_spec, P(None), P(None), P(None), col_split, col_split, col_split, row_split, col_split, col_split, row_split, P(None, None), P('ep', None, 'tp'), P('ep', None, 'tp'), P('ep', 'tp', None))
    out_specs = (row_spec, cache_spec, cache_spec)

    def local_layer(hidden_in, positions, expert_ids, k_cache, v_cache, norm_in, norm_res, norm_post, w_q, w_k, w_v, w_o, w_gate, w_up, w_down, w_router, e_gate, e_up, e_down):
        tokens, dim = hidden_in.shape
        n_local, width = e_gate.shape[0], e_gate.shape[2]
        cache_len, head_dim = k_cache.shape[1], k_cache.shape[3]
        dense_parts = w_down.shape[0] // width
        quarter = dim // n_tp
        n_x = n_ep // 2
        half = tokens // 2
        vmem = pl.BlockSpec(memory_space=pltpu.VMEM)
        hbm = pl.BlockSpec(memory_space=pl.ANY)
        dma = pltpu.SemaphoreType.DMA
        return pl.pallas_call(
            functools.partial(layer_kernel, n_tp, n_ep, 'ep', 'tp'),
            out_shape=(
                jax.ShapeDtypeStruct(hidden_in.shape, BF16),
                jax.ShapeDtypeStruct(k_cache.shape, BF16),
                jax.ShapeDtypeStruct(v_cache.shape, BF16),
            ),
            in_specs=[vmem, vmem, pl.BlockSpec(memory_space=pltpu.SMEM)] + [vmem] * 6 + [hbm] * 12,
            out_specs=(vmem, hbm, hbm),
            scratch_shapes=[
                pltpu.VMEM((n_local, width, dim), BF16),
                pltpu.VMEM((n_local, width, dim), BF16),
                pltpu.VMEM((n_local, width, dim), BF16),
                pltpu.VMEM((2, n_x, tokens, dim), BF16),
                pltpu.VMEM((n_ep, 8, tokens), F32),
                pltpu.VMEM((n_ep, 8, tokens), jnp.int32),
                pltpu.VMEM((n_tp, tokens, quarter), BF16),
                pltpu.VMEM((n_tp - 1, tokens, quarter), BF16),
                pltpu.VMEM((n_tp, tokens, quarter), BF16),
                pltpu.VMEM((tokens, dim), BF16),
                pltpu.VMEM((n_tp, n_x, tokens, quarter), BF16),
                pltpu.VMEM((n_tp, 2, half, quarter), BF16),
                pltpu.VMEM((n_tp, 2, tokens, quarter), BF16),
                pltpu.VMEM((n_tp, tokens, quarter), F32),
                pltpu.VMEM((n_tp - 1, tokens, quarter), BF16),
                pltpu.VMEM((n_tp - 1, tokens, quarter), BF16),
                pltpu.VMEM((n_tp, tokens, quarter), BF16),
                pltpu.VMEM((n_ep, tokens), jnp.int32),
                pltpu.SMEM((n_ep, tokens), jnp.int32),
                dma((9,)), dma((3, n_local)), dma((13,)), dma((13,)), *[dma((n_ep - 1,))] * 4,
                *[dma((n_tp - 1,))] * 4,
                dma((n_tp,)), dma((n_tp,)),
                dma((n_tp, 2)), dma((n_tp, 2)), dma((n_tp, 4)), dma((n_tp, 4)),
                *[dma((n_tp - 1,))] * 4,
            ],
            compiler_params=pltpu.CompilerParams(
                collective_id=0, has_side_effects=True, vmem_limit_bytes=67043328),
        )(
            hidden_in, positions.reshape(1, tokens), positions, expert_ids.T,
            norm_in.reshape(1, dim), norm_res.reshape(1, dim), norm_post.reshape(1, dim), w_router.T,
            jnp.asarray(rope_table(cache_len, head_dim)),
            k_cache, v_cache, w_q, w_k, w_v, w_o,
            w_gate.T.reshape(dense_parts, width, dim), w_up.T.reshape(dense_parts, width, dim),
            w_down.reshape(dense_parts, width, dim),
            jnp.swapaxes(e_gate, 1, 2), jnp.swapaxes(e_up, 1, 2), e_down,
        )

    return jax.shard_map(local_layer, mesh=mesh, in_specs=in_specs, out_specs=out_specs, check_vma=False)
```

time: 325 us -> 97.4 us (0.30)
  waiting for transfers between devices: 117 us -> 0 us
  local copies, waits for them, and re-layouts: 67 us -> 11.1 us
  other arithmetic: 41.4 us -> 0 us
  Pallas kernels: 44.5 us -> 85.4 us
  matrix products: 23.9 us -> 0 us
  between operations: 14.5 us -> 0.64 us
  starting transfers between devices: 13.2 us -> 0 us
    psum x2 -> x0, waiting for transfers between devices: 94.1 us -> none  [the longest x1 62.6 us: local_layer(): expert_sum = lax.psum(expert_part, 'tp')]
    pallas_call x0 -> x1, Pallas kernels: none -> 85.4 us  [local_layer(): pl.pallas_call(functools.partial(layer_kernel, n_tp, n_ep, 'ep', 'tp'), o...]
    another operation x3 -> x0, Pallas kernels: 43 us -> none
    unnamed x37 -> x5, local copies, waits for them, and re-layouts: 33.9 us -> 7.27 us
    dot_general x9 -> x0, matrix products: 23.9 us -> none  [the longest x1 4.87 us: dense_block(): return jnp.dot(act_val, w_down, preferred_element_type=jnp.float32)]
    all_to_all x3 -> x0, waiting for transfers between devices: 23.2 us -> none  [the longest x1 23.2 us: local_layer(): returned = lax.all_to_all(expert_sum, 'ep', 0, 0, tiled=True)]
    gather x9 -> x0, local copies, waits for them, and re-layouts: 18.4 us -> none  [the longest x1 7.08 us: run_experts(): sorted_rows = slot_rows[sort_order]]
    all_to_all x3 -> x0, starting transfers between devices: 12.9 us -> none  [the longest x1 4.53 us: local_layer(): recv_rows = lax.all_to_all(send_rows, 'ep', 0, 0, tiled=True)]
  transfers between devices with their start and end apart: 5 -> 0, of which waited for: 3 -> 0; matrix products, arithmetic and copies ran while one was open for 21% -> 0% of each run, Pallas kernels for 0% -> 0%
where the time goes in v1:
time: 97.4 us; the launch traced here: 97.2 us
  Pallas kernels  85.4 us (88%)
  local copies, waits for them, and re-layouts  11.1 us (11%)
    pallas_call x1, Pallas kernels, local_layer(): pl.pallas_call(functools.partial(layer_kernel, n_tp, n_ep, 'ep', 'tp'), o...  85.4 us
    unnamed x5, local copies, waits for them, and re-layouts  7.27 us

profile of v1, /device:TPU:96, one launch (start us, length us, event | category | flops | bytes accessed | tf_op | source)
XLA Modules:
  0.0 97.2 jit_solution(10117797598979219003)
XLA Ops:
  0.6 1.3 %reshape.28.n_in_ref = bf16[1,2048]{1,0:T(2,128)(2,1)} reshape(bf16[2048]{0:T(1024)(128)(2,1)} %param.25) | data formatting | bytes 8192 | tf_op jit(solution)/shard_map/reshape | solution.py:545
  1.9 1.3 %reshape.29.n_res_ref = bf16[1,2048]{1,0:T(2,128)(2,1)} reshape(bf16[2048]{0:T(1024)(128)(2,1)} %param.26) | data formatting | bytes 8192 | tf_op jit(solution)/shard_map/reshape | solution.py:545
  3.2 1.3 %reshape.30.n_post_ref = bf16[1,2048]{1,0:T(2,128)(2,1)} reshape(bf16[2048]{0:T(1024)(128)(2,1)} %param.27) | data formatting | bytes 8192 | tf_op jit(solution)/shard_map/reshape | solution.py:545
  4.5 85.4 %shard_map.211 = (bf16[128,2048]{1,0:T(8,128)(2,1)}, bf16[128,16,4,128]{3,2,1,0:T(4,128)(2,1)}, bf16[128,16,4,128]{3,2,1,0:T(4,128)(2,1)}) custom-call(bf16[128,2048]{1,0:T(8,128)(2,1)} %x_ref.1, s32[1,128]{1,0:T(1,128)} %bitcast.18, s32[128]{0:T(128)} %pos_smem.1, s32[2,128]{1,0:T(2,128)} %bitcast.19, bf16[1,2048]{1,0:T(2,128)(2,1)} %reshape.28.n_in_ref, ...), custom_call_target="tpu_custom_call" | custom-call | tf_op jit(solution)/shard_map/pallas_call | solution.py:506
  89.9 1.9 %copy.26 = bf16[128,2048]{1,0:T(8,128)(2,1)} copy(bf16[128,2048]{1,0:T(8,128)(2,1)} %get-tuple-element.6) | data formatting | bytes 1048576
  91.8 0.0 copy-start
  91.8 4.1 %copy.27 = bf16[128,16,4,128]{3,2,1,0:T(4,128)(2,1)} copy(bf16[128,16,4,128]{3,2,1,0:T(4,128)(2,1)} %get-tuple-element.7) | data formatting | bytes 4194304
  95.8 0.0 copy-done
  95.8 1.3 %copy.28 = bf16[128,16,4,128]{3,2,1,0:T(4,128)(2,1)} copy(bf16[128,16,4,128]{3,2,1,0:T(4,128)(2,1)S(1)} %copy-done) | data formatting | bytes 4194304
Async XLA Ops:
  91.8 4.1 %copy-start = (bf16[128,16,4,128]{3,2,1,0:T(4,128)(2,1)S(1)}, bf16[128,16,4,128]{3,2,1,0:T(4,128)(2,1)}, u32[]{:S(2)}) copy-start(bf16[128,16,4,128]{3,2,1,0:T(4,128)(2,1)} %get-tuple-element.8) | copy-start | bytes 6291460

commit v2 on v1

--- a/solution.py
+++ b/solution.py
@@ -17,6 +17,11 @@
 ALIGN = 16
 
 
+def as_row(gains):
+    wide = gains.astype(F32)
+    return jnp.concatenate([wide[i:i + 1, :] for i in range(wide.shape[0])], axis=1)
+
+
 def rms_norm(values, gain_row):
     wide_vals = values.astype(F32)
     inv_rms = lax.rsqrt(jnp.mean(wide_vals * wide_vals, axis=-1, keepdims=True) + NORM_EPS)
@@ -51,9 +56,9 @@
 
 def layer_kernel(
     n_tp, n_ep, ep_axis, tp_axis,
-    x_ref, pos_row_ref, pos_smem, ids_ref, n_in_ref, n_res_ref, n_post_ref, w_router_ref, rope_ref,
+    x_ref, pos_row_ref, ids_ref, n_in_ref, n_res_ref, n_post_ref, w_router_ref, rope_ref,
     k_hbm, v_hbm, wq_hbm, wk_hbm, wv_hbm, wo_hbm, wg_hbm, wu_hbm, wd_hbm, eg_hbm, eu_hbm, ed_hbm,
-    out_ref, k_out, v_out,
+    out_ref, k_new, v_new,
     eg, eu, ed, rows_all, meta, all_ids, part_q, part_in, h_q, c_buf, d_in, r1_in, r2_in, dense_q, fin_q, fin_in, out_q,
     sched_v, sched,
     w_sem, e_sem, ag_send, ag_recv, m_send, m_recv, i_send, i_recv, a_send, a_recv, h_send, h_recv, d_send, d_recv,
@@ -64,7 +69,9 @@
     n_x = n_ep // 2
     half = tokens // 2
     n_local, width = eg.shape[0], eg.shape[1]
-    cache_len, heads, head_dim = k_hbm.shape[1], k_hbm.shape[2], k_hbm.shape[3]
+    head_dim = k_hbm.shape[1]
+    heads = wq_hbm.shape[1] // head_dim
+    cache_len = k_hbm.shape[0] // (tokens * heads)
     n_blocks = n_ep
     all_rows = n_blocks * tokens
     n_sorted = -(-(4 * tokens + n_local * (ALIGN - 1)) // 128) * 128
@@ -122,7 +129,7 @@
     for k in range(1, n_tp):
         pl.semaphore_signal(barrier, inc=1, device_id=tp_peer(k), device_id_type=MESH)
 
-    def attention_phase(wq, wk, wv, wo, kc, vc, q_s, k_s, v_s, o_s):
+    def attention_phase(wq, wk, wv, wo, kc, vc, q_s, k_s, v_s, o_s, pos_s):
         loads = [
             pltpu.make_async_copy(src, dst, w_sem.at[i])
             for i, (src, dst) in enumerate(
@@ -131,7 +138,7 @@
         for load in loads:
             load.start()
 
-        moe_in = rms_norm(x_ref[...], n_post_ref[...])
+        moe_in = rms_norm(x_ref[...], as_row(n_post_ref[...]))
         rows_all[core, chip] = moe_in
         logits = dot_nt(w_router_ref[...], moe_in)
         shifted = jnp.exp(logits - jnp.max(logits, axis=0, keepdims=True))
@@ -163,7 +170,7 @@
         for send in sends:
             send.start()
 
-        normed = rms_norm(x_ref[...], n_in_ref[...])
+        normed = rms_norm(x_ref[...], as_row(n_in_ref[...]))
         pos_col = jnp.transpose(jnp.broadcast_to(pos_row_ref[...].astype(F32), (tokens, tokens)))
         cosine = jnp.zeros((tokens, head_dim), F32)
         sine = jnp.zeros((tokens, head_dim), F32)
@@ -174,14 +181,18 @@
         def rotated(values):
             return values * cosine + pltpu.roll(values, head_dim // 2, 1) * sine
 
-        for load, weights, dest, turn in (
-            (loads[0], wq, q_s, True), (loads[1], wk, k_s, True), (loads[2], wv, v_s, False)):
+        for head in range(heads):
+            pos_s[pl.ds(head, tokens, stride=heads), :] = pos_col
+        for load, weights, dest in ((loads[0], wq, q_s), (loads[1], wk, k_s), (loads[2], wv, v_s)):
             load.wait()
             proj = dot_nn(normed, weights[...])
             for head in range(heads):
                 values = proj[:, head * head_dim:(head + 1) * head_dim]
-                values = rotated(values) if turn else values
-                dest[:, head, :] = values.astype(BF16).astype(F32)
+                if dest is not v_s:
+                    values = rotated(values)
+                dest[pl.ds(head, tokens, stride=heads), :] = values.astype(BF16).astype(F32)
+        k_new[...] = k_s[...].astype(BF16)
+        v_new[...] = v_s[...].astype(BF16)
 
         for e in range(n_local):
             pltpu.make_async_copy(eg_hbm.at[e], eg.at[e], e_sem.at[0, e]).start()
@@ -190,69 +201,61 @@
 
         loads[3].wait()
         loads[4].wait()
-        slot = lax.broadcasted_iota(jnp.int32, (cache_len, heads, head_dim), 0)
-        slot_one = lax.broadcasted_iota(jnp.int32, (cache_len, heads, 1), 0)
-        unroll = 4
-
-        def attend(group, carry):
-            for i in range(unroll):
-                t = group * unroll + i
-                at = pos_smem[t]
-                keys = jnp.where(slot == at, k_s[t][None], kc[t].astype(F32))
-                kc[t] = keys.astype(BF16)
-                scores = jnp.sum(keys * q_s[t][None], axis=-1, keepdims=True) * (head_dim ** -0.5)
-                scores = jnp.where(slot_one <= at, scores, -jnp.inf)
-                weights = jnp.exp(scores - jnp.max(scores, axis=0, keepdims=True))
-                weights = weights / jnp.sum(weights, axis=0, keepdims=True)
-                weights = weights.astype(BF16).astype(F32)
-                vals = jnp.where(slot == at, v_s[t][None], vc[t].astype(F32))
-                vc[t] = vals.astype(BF16)
-                visible_vals = jnp.where(slot <= at, vals, 0.0)
-                o_s[t] = jnp.sum(weights * visible_vals, axis=0)
+        group = 16 // heads
+        q_rows, slots = 16, group * cache_len * heads
+        shape = (q_rows, slots)
+        row, col = lax.broadcasted_iota(jnp.int32, shape, 0), lax.broadcasted_iota(jnp.int32, shape, 1)
+        own_rows = jnp.logical_and(row // heads == col // (cache_len * heads), row % heads == col % heads)
+        slot = jnp.where(own_rows, col // heads % cache_len, cache_len).astype(F32)
+
+        def attend(g, carry):
+            rows = pl.ds(pl.multiple_of(g * q_rows, q_rows), q_rows)
+            wide_rows = pl.ds(pl.multiple_of(g * slots, slots), slots)
+            query, key = q_s[rows, :], k_s[rows, :]
+            at = pos_s[rows, :]
+            scores = dot_nt(query.astype(BF16), kc[wide_rows, :]) * (head_dim ** -0.5)
+            scores = jnp.where(slot < jnp.concatenate([at] * (slots // 128), axis=1), scores, -jnp.inf)
+            score_new = jnp.sum(query * key, axis=1, keepdims=True) * (head_dim ** -0.5)
+            top = jnp.maximum(jnp.max(scores, axis=1, keepdims=True), score_new)
+            weights, weight_new = jnp.exp(scores - top), jnp.exp(score_new - top)
+            total = jnp.sum(weights, axis=1, keepdims=True) + weight_new
+            mix = dot_nn((weights / total).astype(BF16), vc[wide_rows, :])
+            o_s[rows, :] = mix + (weight_new / total).astype(BF16).astype(F32) * v_s[rows, :]
             return carry
 
-        lax.fori_loop(0, tokens // unroll, attend, 0)
-        stores = [pltpu.make_async_copy(kc, k_out, w_sem.at[6]), pltpu.make_async_copy(vc, v_out, w_sem.at[7])]
-        for store in stores:
-            store.start()
+        lax.fori_loop(0, tokens // group, attend, 0, unroll=8)
 
         forward_first()
 
-        mixed = jnp.concatenate([o_s[:, head, :] for head in range(heads)], axis=1).astype(BF16)
+        mixed = jnp.concatenate(
+            [o_s[pl.ds(head, tokens, stride=heads), :] for head in range(heads)], axis=1).astype(BF16)
         loads[5].wait()
         for q in range(n_tp):
             part_q[q] = dot_nn(mixed, wo[:, q * quarter:(q + 1) * quarter]).astype(BF16)
         for k in range(1, n_tp):
             send = remote(part_q.at[(tp + k) % n_tp], part_in.at[k - 1], a_send.at[k - 1], a_recv.at[k - 1], tp_peer(k))
             send.start()
-        for store in stores:
-            store.wait()
 
     pl.run_scoped(
         attention_phase,
         *[pltpu.VMEM((dim, heads * head_dim), BF16)] * 3,
         pltpu.VMEM((heads * head_dim, dim), BF16),
-        *[pltpu.VMEM((tokens, cache_len, heads, head_dim), BF16)] * 2,
-        *[pltpu.VMEM((tokens, heads, head_dim), F32)] * 4,
+        *[pltpu.VMEM(k_hbm.shape, BF16)] * 2,
+        *[pltpu.VMEM((tokens * heads, head_dim), F32)] * 5,
     )
 
-    forward(2, left, high)
-    forward(4, right, low)
-
-    mine = pl.ds(pl.multiple_of(tp * quarter, quarter), quarter)
-    for k in range(1, n_tp):
-        arrived(part_in.at[k - 1], a_recv.at[k - 1])
-    attn_sum = part_q[tp].astype(F32)
-    for k in range(1, n_tp):
-        attn_sum = attn_sum + part_in[k - 1].astype(F32)
-    h_q[tp] = (x_ref[:, mine].astype(F32) + attn_sum).astype(BF16)
-    for k in range(1, n_tp):
-        remote(h_q.at[tp], h_q.at[tp], h_send.at[k - 1], h_recv.at[k - 1], tp_peer(k)).start()
-
-    forward(5, far, low)
-    forward(6, far, high)
-
-    def expert_phase(xs, sort, unsort, z, ys, y_sorted, weight_sorted):
+    def attention_sum():
+        mine = pl.ds(pl.multiple_of(tp * quarter, quarter), quarter)
+        for k in range(1, n_tp):
+            arrived(part_in.at[k - 1], a_recv.at[k - 1])
+        attn_sum = part_q[tp].astype(F32)
+        for k in range(1, n_tp):
+            attn_sum = attn_sum + part_in[k - 1].astype(F32)
+        h_q[tp] = (x_ref[:, mine].astype(F32) + attn_sum).astype(BF16)
+        for k in range(1, n_tp):
+            remote(h_q.at[tp], h_q.at[tp], h_send.at[k - 1], h_recv.at[k - 1], tp_peer(k)).start()
+
+    def expert_phase(xs, sort, unsort, z, ys, y_sorted, weight_sorted, place_s, weight_s, act_s):
         for k in range(1, n_ep):
             source = (ep + n_ep - k) % n_ep
             arrived(meta.at[(source % 2) * n_x + source // 2], m_recv.at[k - 1])
@@ -295,12 +298,18 @@
         to_scalar = pltpu.make_async_copy(sched_v, sched, w_sem.at[8])
         to_scalar.start()
 
+        place_s[...] = place
+        weight_s[...] = weight
         row_id = lax.broadcasted_iota(jnp.int32, (n_sorted, tokens), 0)
         weight_rows = jnp.zeros((n_sorted, tokens), F32)
-        for j in range(n_blocks):
-            match = row_id == place[j:j + 1, :]
-            sort[:, j * tokens:(j + 1) * tokens] = jnp.where(match, 1.0, 0.0).astype(BF16)
-            weight_rows = weight_rows + jnp.where(match, weight[j:j + 1, :], 0.0)
+        spots = (chip, left, right, far)
+        for n, spot in enumerate(spots):
+            for c in range(2):
+                source = pl.ds(c * n_x + spot, 1)
+                match = row_id == place_s[source, :]
+                first_col = (2 * n + c) * tokens
+                sort[:, first_col:first_col + tokens] = jnp.where(match, 1.0, 0.0).astype(BF16)
+                weight_rows = weight_rows + jnp.where(match, weight_s[source, :], 0.0)
         weight_sorted[0:n_sorted, :] = jnp.broadcast_to(
             jnp.sum(weight_rows, axis=1, keepdims=True), (n_sorted, 128))
         weight_sorted[n_sorted:, :] = jnp.zeros((ROWS, 128), F32)
@@ -311,23 +320,40 @@
             unsort[j * tokens:(j + 1) * tokens, :] = jnp.where(
                 column_id == place_cols[:, j:j + 1], 1.0, 0.0).astype(BF16)
 
+        forward(2, left, high)
+        forward(4, right, low)
+        attention_sum()
+
+        def add_rows(numbers):
+            def one(i, carry):
+                cols = pl.ds(pl.multiple_of(i * 256, 256), 256)
+                total = None
+                for n in numbers:
+                    rows = rows_all[:, spots[n], :, cols].reshape(2 * tokens, 256)
+                    part = dot_nn(sort[:, 2 * n * tokens:(2 * n + 2) * tokens], rows)
+                    total = part if total is None else total + part
+                if numbers[0] > 0:
+                    total = total + xs[0:n_sorted, cols].astype(F32)
+                xs[0:n_sorted, cols] = total.astype(BF16)
+                return carry
+
+            lax.fori_loop(0, dim // 256, one, 0, unroll=2)
+
         arrived(rows_all.at[other, chip], ag_recv.at[0])
-        for index, spot, part in ((1, left, low), (2, left, high), (3, right, high), (4, right, low), (5, far, low), (6, far, high)):
+        for index, spot, part in ((1, left, low), (2, left, high), (3, right, high), (4, right, low)):
             arrived(rows_all.at[other, spot, part], ag_recv.at[index + 6])
+        add_rows((0, 1, 2))
+        forward(5, far, low)
+        forward(6, far, high)
+        for index, part in ((5, low), (6, high)):
+            arrived(rows_all.at[other, far, part], ag_recv.at[index + 6])
+        add_rows((3,))
         for index in range(1, 13):
             sent(rows_all.at[core, chip, low], ag_send.at[index])
         sent(rows_all.at[core, chip], ag_send.at[0])
         for k in range(1, n_ep):
             sent(meta.at[core * n_x + chip], m_send.at[k - 1])
             sent(all_ids.at[core * n_x + chip], i_send.at[k - 1])
-
-        def sort_columns(i, carry):
-            cols = pl.ds(pl.multiple_of(i * 256, 256), 256)
-            rows = rows_all[:, :, :, cols].reshape(all_rows, 256)
-            xs[0:n_sorted, cols] = dot_nn(sort[...], rows).astype(BF16)
-            return carry
-
-        lax.fori_loop(0, dim // 256, sort_columns, 0)
         to_scalar.wait()
         for e in range(n_local):
             pltpu.make_async_copy(eg_hbm.at[e], eg.at[e], e_sem.at[0, e]).wait()
@@ -340,7 +366,7 @@
             z[step] = jnp.transpose(act).astype(BF16)
             return carry
 
-        lax.fori_loop(0, n_steps, gate_up, 0)
+        lax.fori_loop(0, n_steps, gate_up, 0, unroll=3)
 
         for p in range(dense_parts):
             pltpu.make_async_copy(wg_hbm.at[p], eg.at[p], w_sem.at[p]).start()
@@ -349,7 +375,7 @@
         for e in range(n_local):
             pltpu.make_async_copy(ed_hbm.at[e], ed.at[e], e_sem.at[2, e]).wait()
 
-        for i in range(n_tp):
+        def compute(i):
             cols = columns(i)
 
             def down(step, carry):
@@ -360,22 +386,36 @@
                 ys[pl.ds(pl.multiple_of(step * ROWS, ROWS), ROWS), :] = jnp.concatenate(scaled, axis=1).astype(BF16)
                 return carry
 
-            lax.fori_loop(0, n_steps, down, 0)
+            lax.fori_loop(0, n_steps, down, 0, unroll=3)
 
             def regroup(b, carry):
-                y_sorted[pl.ds(pl.multiple_of(b * ALIGN, ALIGN), ALIGN), :] = ys[
-                    pl.ds(sched[2, b] * ALIGN, ALIGN), :]
+                y_sorted[pl.ds(pl.multiple_of(b * ALIGN, ALIGN), ALIGN), :] = ys[pl.ds(sched[2, b] * ALIGN, ALIGN), :]
                 return carry
 
-            lax.fori_loop(0, n_sorted // ALIGN, regroup, 0)
+            lax.fori_loop(0, n_sorted // ALIGN, regroup, 0, unroll=8)
             for c in range(2):
                 back = dot_nn(unsort[c * n_x * tokens:(c + 1) * n_x * tokens, :], y_sorted[...])
                 rows_all[c, :, :, cols] = back.astype(BF16).reshape(n_x, tokens, quarter)
             remote(rows_all.at[other, :, :, cols], d_in.at[i], d_send.at[i], d_recv.at[i], partner).start()
-            if i >= 1:
-                pair_sum(i - 1)
-            if i >= 2:
-                ring_sum(i - 2)
+
+        compute(0)
+        dense_gate_up(act_s)
+        pair_sum(0)
+        compute(1)
+        ring_sum(0)
+        dense_down(act_s)
+        pair_sum(1)
+        compute(2)
+        ring_sum(1)
+        finish(0)
+        pair_sum(2)
+        compute(3)
+        ring_sum(2)
+        finish(1)
+        pair_sum(3)
+        ring_sum(3)
+        finish(2)
+        finish(3)
 
     def columns(i):
         return pl.ds(pl.multiple_of(((tp + 1 + i) % n_tp) * quarter, quarter), quarter)
@@ -402,41 +442,29 @@
             rows_all[core, left, high, cols].astype(F32) + r1_in[i, 1].astype(F32)).astype(BF16)
         remote(rows_all.at[core, left, high, cols], r2_in.at[i, 1, high], r2_send.at[i, 3], r2_recv.at[i, 3], on_ring(left)).start()
 
-    pl.run_scoped(
-        expert_phase,
-        pltpu.VMEM((n_sorted + ROWS, dim), BF16),
-        pltpu.VMEM((n_sorted, all_rows), BF16),
-        pltpu.VMEM((all_rows, n_sorted), BF16),
-        pltpu.VMEM((n_steps, ROWS, width), BF16),
-        pltpu.VMEM((n_steps * ROWS, quarter), BF16),
-        pltpu.VMEM((n_sorted, quarter), BF16),
-        pltpu.VMEM((n_sorted + ROWS, 128), F32),
-    )
-    pair_sum(n_tp - 1)
-    ring_sum(n_tp - 2)
-
-    for k in range(1, n_tp):
-        source = (tp + n_tp - k) % n_tp
-        arrived(h_q.at[source], h_recv.at[k - 1])
-    hidden_mid = jnp.concatenate([h_q[q] for q in range(n_tp)], axis=1)
-    c_buf[...] = rms_norm(hidden_mid, n_res_ref[...])
-    acts = []
-    for p in range(dense_parts):
-        pltpu.make_async_copy(wg_hbm.at[p], eg.at[p], w_sem.at[p]).wait()
-        pltpu.make_async_copy(wu_hbm.at[p], eu.at[p], w_sem.at[2 + p]).wait()
-        act = jax.nn.silu(dot_nt(eg[p], c_buf[...])) * dot_nt(eu[p], c_buf[...])
-        acts.append(jnp.transpose(act).astype(BF16))
-    for p in range(dense_parts):
-        pltpu.make_async_copy(wd_hbm.at[p], eg.at[dense_parts + p], w_sem.at[4 + p]).wait()
-    for q in range(n_tp):
-        cols = slice(q * quarter, (q + 1) * quarter)
-        dense = dot_nn(acts[0], eg[dense_parts, :, cols])
-        for p in range(1, dense_parts):
-            dense = dense + dot_nn(acts[p], eg[dense_parts + p, :, cols])
-        dense_q[q] = dense
-    ring_sum(n_tp - 1)
-
-    for i in range(n_tp):
+    def dense_gate_up(act_s):
+        for k in range(1, n_tp):
+            source = (tp + n_tp - k) % n_tp
+            arrived(h_q.at[source], h_recv.at[k - 1])
+        hidden_mid = jnp.concatenate([h_q[q] for q in range(n_tp)], axis=1)
+        c_buf[...] = rms_norm(hidden_mid, as_row(n_res_ref[...]))
+        for p in range(dense_parts):
+            pltpu.make_async_copy(wg_hbm.at[p], eg.at[p], w_sem.at[p]).wait()
+            pltpu.make_async_copy(wu_hbm.at[p], eu.at[p], w_sem.at[2 + p]).wait()
+            act = jax.nn.silu(dot_nt(eg[p], c_buf[...])) * dot_nt(eu[p], c_buf[...])
+            act_s[p] = jnp.transpose(act).astype(BF16)
+
+    def dense_down(act_s):
+        for p in range(dense_parts):
+            pltpu.make_async_copy(wd_hbm.at[p], eg.at[dense_parts + p], w_sem.at[4 + p]).wait()
+        for q in range(n_tp):
+            cols = slice(q * quarter, (q + 1) * quarter)
+            dense = dot_nn(act_s[0], eg[dense_parts, :, cols])
+            for p in range(1, dense_parts):
+                dense = dense + dot_nn(act_s[p], eg[dense_parts + p, :, cols])
+            dense_q[q] = dense
+
+    def finish(i):
         q = (tp + 1 + i) % n_tp
         cols = columns(i)
         arrived(r2_in.at[i, 0, high], r2_recv.at[i, 0])
@@ -452,6 +480,20 @@
                 arrived(fin_in.at[k - 1], f_recv.at[k - 1])
                 part = part + fin_in[k - 1].astype(F32)
             out_q[tp] = (h_q[tp].astype(F32) + part).astype(BF16)
+
+    pl.run_scoped(
+        expert_phase,
+        pltpu.VMEM((n_sorted + ROWS, dim), BF16),
+        pltpu.VMEM((n_sorted, all_rows), BF16),
+        pltpu.VMEM((all_rows, n_sorted), BF16),
+        pltpu.VMEM((n_steps, ROWS, width), BF16),
+        pltpu.VMEM((n_steps * ROWS, quarter), BF16),
+        pltpu.VMEM((n_sorted, quarter), BF16),
+        pltpu.VMEM((n_sorted + ROWS, 128), F32),
+        pltpu.VMEM((n_blocks, tokens), jnp.int32),
+        pltpu.VMEM((n_blocks, tokens), F32),
+        pltpu.VMEM((dense_parts, tokens, width), BF16),
+    )
     for k in range(1, n_tp):
         remote(out_q.at[tp], out_q.at[tp], o_send.at[k - 1], o_recv.at[k - 1], tp_peer(k)).start()
 
@@ -475,6 +517,30 @@
         sent(part_in.at[k - 1], o_send.at[k - 1])
 
 
+def cache_kernel(pieces, pos, hidden_ref, k_new, v_new, k_hbm, v_hbm, out_ref, k_out, v_out, k_buf, v_buf, in_sem, out_sem):
+    size = k_buf.shape[0] // pieces
+    both = ((k_hbm, k_buf, k_out, k_new), (v_hbm, v_buf, v_out, v_new))
+    loads = [
+        [pltpu.make_async_copy(src.at[pl.ds(i * size, size)], buf.at[pl.ds(i * size, size)], in_sem.at[n, i])
+         for n, (src, buf, _, _) in enumerate(both)] for i in range(pieces)]
+    stores = [
+        [pltpu.make_async_copy(buf.at[pl.ds(i * size, size)], dst.at[pl.ds(i * size, size)], out_sem.at[n, i])
+         for n, (_, buf, dst, _) in enumerate(both)] for i in range(pieces)]
+    for pair in loads:
+        for load in pair:
+            load.start()
+    out_ref[...] = hidden_ref[...]
+    for i in range(pieces):
+        for n, (_, buf, _, new) in enumerate(both):
+            loads[i][n].wait()
+            for t in range(i * size, (i + 1) * size):
+                buf[t, pos[t]] = new[t]
+            stores[i][n].start()
+    for pair in stores:
+        for store in pair:
+            store.wait()
+
+
 def rope_table(cache_len, head_dim):
     freq = 1.0 / (ROPE_BASE ** (np.arange(0, head_dim, 2, dtype=np.float32) / np.float32(head_dim)))
     angle = np.arange(cache_len, dtype=np.float32)[:, None] * freq.astype(np.float32)[None, :]
@@ -495,7 +561,7 @@
     def local_layer(hidden_in, positions, expert_ids, k_cache, v_cache, norm_in, norm_res, norm_post, w_q, w_k, w_v, w_o, w_gate, w_up, w_down, w_router, e_gate, e_up, e_down):
         tokens, dim = hidden_in.shape
         n_local, width = e_gate.shape[0], e_gate.shape[2]
-        cache_len, head_dim = k_cache.shape[1], k_cache.shape[3]
+        cache_len, heads, head_dim = k_cache.shape[1:]
         dense_parts = w_down.shape[0] // width
         quarter = dim // n_tp
         n_x = n_ep // 2
@@ -503,15 +569,15 @@
         vmem = pl.BlockSpec(memory_space=pltpu.VMEM)
         hbm = pl.BlockSpec(memory_space=pl.ANY)
         dma = pltpu.SemaphoreType.DMA
-        return pl.pallas_call(
+        hidden, k_new, v_new = pl.pallas_call(
             functools.partial(layer_kernel, n_tp, n_ep, 'ep', 'tp'),
             out_shape=(
                 jax.ShapeDtypeStruct(hidden_in.shape, BF16),
-                jax.ShapeDtypeStruct(k_cache.shape, BF16),
-                jax.ShapeDtypeStruct(v_cache.shape, BF16),
+                jax.ShapeDtypeStruct((tokens * heads, head_dim), BF16),
+                jax.ShapeDtypeStruct((tokens * heads, head_dim), BF16),
             ),
-            in_specs=[vmem, vmem, pl.BlockSpec(memory_space=pltpu.SMEM)] + [vmem] * 6 + [hbm] * 12,
-            out_specs=(vmem, hbm, hbm),
+            in_specs=[vmem] * 8 + [hbm] * 12,
+            out_specs=(vmem, vmem, vmem),
             scratch_shapes=[
                 pltpu.VMEM((n_local, width, dim), BF16),
                 pltpu.VMEM((n_local, width, dim), BF16),
@@ -541,13 +607,27 @@
             compiler_params=pltpu.CompilerParams(
                 collective_id=0, has_side_effects=True, vmem_limit_bytes=67043328),
         )(
-            hidden_in, positions.reshape(1, tokens), positions, expert_ids.T,
-            norm_in.reshape(1, dim), norm_res.reshape(1, dim), norm_post.reshape(1, dim), w_router.T,
+            hidden_in, positions.reshape(1, tokens), expert_ids.T,
+            norm_in.reshape(-1, 128), norm_res.reshape(-1, 128), norm_post.reshape(-1, 128), w_router.T,
             jnp.asarray(rope_table(cache_len, head_dim)),
-            k_cache, v_cache, w_q, w_k, w_v, w_o,
+            k_cache.reshape(-1, head_dim), v_cache.reshape(-1, head_dim), w_q, w_k, w_v, w_o,
             w_gate.T.reshape(dense_parts, width, dim), w_up.T.reshape(dense_parts, width, dim),
             w_down.reshape(dense_parts, width, dim),
             jnp.swapaxes(e_gate, 1, 2), jnp.swapaxes(e_up, 1, 2), e_down,
         )
+        return pl.pallas_call(
+            functools.partial(cache_kernel, 8),
+            out_shape=(
+                jax.ShapeDtypeStruct(hidden_in.shape, BF16),
+                jax.ShapeDtypeStruct(k_cache.shape, BF16),
+                jax.ShapeDtypeStruct(v_cache.shape, BF16),
+            ),
+            in_specs=[pl.BlockSpec(memory_space=pltpu.SMEM), vmem, vmem, vmem, hbm, hbm],
+            out_specs=(vmem, hbm, hbm),
+            scratch_shapes=[
+                pltpu.VMEM(k_cache.shape, BF16), pltpu.VMEM(v_cache.shape, BF16),
+                dma((2, 8)), dma((2, 8)),
+            ],
+        )(positions, hidden, k_new.reshape(tokens, heads, head_dim), v_new.reshape(tokens, heads, head_dim), k_cache, v_cache)
 
     return jax.shard_map(local_layer, mesh=mesh, in_specs=in_specs, out_specs=out_specs, check_vma=False)

time: 97.4 us -> 88.4 us (0.908)
  local copies, waits for them, and re-layouts: 11.1 us -> 0 us
  Pallas kernels: 85.4 us -> 87.5 us
    unnamed x5 -> x0, local copies, waits for them, and re-layouts: 7.27 us -> none
    pallas_call x0 -> x1, Pallas kernels: none -> 5.75 us  [local_layer(): pl.pallas_call(functools.partial(cache_kernel, 8), out_shape=(jax.ShapeDt...]
    reshape x3 -> x0, local copies, waits for them, and re-layouts: 3.87 us -> none  [the longest x1 1.29 us: local_layer(): norm_in.reshape(1, dim)]
    pallas_call x1, Pallas kernels: 85.4 us -> 81.7 us  [local_layer(): pl.pallas_call(functools.partial(layer_kernel, n_tp, n_ep, 'ep', 'tp'), o...]
where the time goes in v2:
time: 88.4 us; the launch traced here: 88.3 us
  Pallas kernels  87.5 us (99%)
    pallas_call x1, Pallas kernels, local_layer(): pl.pallas_call(functools.partial(layer_kernel, n_tp, n_ep, 'ep', 'tp'), o...  81.7 us
    pallas_call x1, Pallas kernels, local_layer(): pl.pallas_call(functools.partial(cache_kernel, 8), out_shape=(jax.ShapeDt...  5.75 us

profile of v2, /device:TPU:96, one launch (start us, length us, event | category | flops | bytes accessed | tf_op | source)
XLA Modules:
  0.0 88.3 jit_solution(5961331235278794835)
XLA Ops:
  0.6 81.7 %shard_map.211 = (bf16[128,2048]{1,0:T(8,128)(2,1)}, bf16[512,128]{1,0:T(8,128)(2,1)}, bf16[512,128]{1,0:T(8,128)(2,1)}) custom-call(bf16[128,2048]{1,0:T(8,128)(2,1)} %x_ref.1, s32[1,128]{1,0:T(1,128)} %bitcast.32, s32[2,128]{1,0:T(2,128)} %bitcast.33, bf16[16,128]{1,0:T(8,128)(2,1)} %bitcast.29, bf16[16,128]{1,0:T(8,128)(2,1)} %bitcast.30, ...), custom_call_target="tpu_custom_call" | custom-call | tf_op jit(solution)/shard_map/pallas_call | solution.py:572
  82.4 5.8 %shard_map.212 = (bf16[128,2048]{1,0:T(8,128)(2,1)}, bf16[128,16,4,128]{3,2,1,0:T(4,128)(2,1)}, bf16[128,16,4,128]{3,2,1,0:T(4,128)(2,1)}) custom-call(s32[128]{0:T(128)} %pos.1, bf16[128,2048]{1,0:T(8,128)(2,1)} %get-tuple-element.6.hidden_ref, bf16[128,4,128]{2,1,0:T(4,128)(2,1)} %bitcast.27, bf16[128,4,128]{2,1,0:T(4,128)(2,1)} %bitcast.28, ...), custom_call_target="tpu_custom_call" | custom-call | tf_op jit(solution)/shard_map/pallas_call | solution.py:618

commit v3 on v2

--- a/solution.py
+++ b/solution.py
@@ -208,22 +208,31 @@
         own_rows = jnp.logical_and(row // heads == col // (cache_len * heads), row % heads == col % heads)
         slot = jnp.where(own_rows, col // heads % cache_len, cache_len).astype(F32)
 
-        def attend(g, carry):
-            rows = pl.ds(pl.multiple_of(g * q_rows, q_rows), q_rows)
-            wide_rows = pl.ds(pl.multiple_of(g * slots, slots), slots)
-            query, key = q_s[rows, :], k_s[rows, :]
-            at = pos_s[rows, :]
-            scores = dot_nt(query.astype(BF16), kc[wide_rows, :]) * (head_dim ** -0.5)
-            scores = jnp.where(slot < jnp.concatenate([at] * (slots // 128), axis=1), scores, -jnp.inf)
-            score_new = jnp.sum(query * key, axis=1, keepdims=True) * (head_dim ** -0.5)
-            top = jnp.maximum(jnp.max(scores, axis=1, keepdims=True), score_new)
-            weights, weight_new = jnp.exp(scores - top), jnp.exp(score_new - top)
-            total = jnp.sum(weights, axis=1, keepdims=True) + weight_new
-            mix = dot_nn((weights / total).astype(BF16), vc[wide_rows, :])
-            o_s[rows, :] = mix + (weight_new / total).astype(BF16).astype(F32) * v_s[rows, :]
+        batch = 8
+
+        def attend(step, carry):
+            rows = [pl.ds(pl.multiple_of((step * batch + g) * q_rows, q_rows), q_rows) for g in range(batch)]
+            wide_rows = [pl.ds(pl.multiple_of((step * batch + g) * slots, slots), slots) for g in range(batch)]
+            query = [q_s[r, :] for r in rows]
+            at = [pos_s[r, :] for r in rows]
+            scores = [dot_nt(q.astype(BF16), kc[w, :]) * (head_dim ** -0.5) for q, w in zip(query, wide_rows)]
+            score_new = [
+                jnp.sum(q * k_s[r, :], axis=1, keepdims=True) * (head_dim ** -0.5) for q, r in zip(query, rows)]
+            scores = [
+                jnp.where(slot < jnp.concatenate([p] * (slots // 128), axis=1), x, -jnp.inf) for x, p in zip(scores, at)]
+            top = [jnp.maximum(jnp.max(x, axis=1, keepdims=True), n) for x, n in zip(scores, score_new)]
+            weights = [jnp.exp(x - t) for x, t in zip(scores, top)]
+            weight_new = [jnp.exp(n - t) for n, t in zip(score_new, top)]
+            total = [jnp.sum(w, axis=1, keepdims=True) + n for w, n in zip(weights, weight_new)]
+            weights = [(w / t).astype(BF16) for w, t in zip(weights, total)]
+            weight_new = [(n / t).astype(BF16).astype(F32) for n, t in zip(weight_new, total)]
+            mix = [dot_nn(w, vc[r, :]) for w, r in zip(weights, wide_rows)]
+            mix = [m + n * v_s[r, :] for m, n, r in zip(mix, weight_new, rows)]
+            for m, r in zip(mix, rows):
+                o_s[r, :] = m
             return carry
 
-        lax.fori_loop(0, tokens // group, attend, 0, unroll=8)
+        lax.fori_loop(0, tokens // group // batch, attend, 0)
 
         forward_first()
 
@@ -494,8 +503,21 @@
         pltpu.VMEM((n_blocks, tokens), F32),
         pltpu.VMEM((dense_parts, tokens, width), BF16),
     )
-    for k in range(1, n_tp):
-        remote(out_q.at[tp], out_q.at[tp], o_send.at[k - 1], o_recv.at[k - 1], tp_peer(k)).start()
+    before, after, across = (tp + n_tp - 1) % n_tp, (tp + 1) % n_tp, (tp + 2) % n_tp
+    up, down = tp_peer(1), tp_peer(n_tp - 1)
+
+    def pass_on(index, place, rows, device):
+        block = out_q.at[place, rows]
+        remote(block, block, o_send.at[index], o_recv.at[index], device).start()
+
+    pass_on(0, tp, low, up)
+    pass_on(1, tp, high, down)
+    pass_on(2, tp, high, up)
+    pass_on(3, tp, low, down)
+    arrived(out_q.at[before, low], o_recv.at[0])
+    pass_on(4, before, low, up)
+    arrived(out_q.at[after, high], o_recv.at[1])
+    pass_on(5, after, high, down)
 
     for i in range(n_tp):
         cols = columns(i)
@@ -508,37 +530,53 @@
         sent(part_in.at[k - 1], a_send.at[k - 1])
         sent(part_in.at[k - 1], h_send.at[k - 1])
         sent(part_in.at[k - 1], f_send.at[k - 1])
-    for k in range(1, n_tp):
-        source = (tp + n_tp - k) % n_tp
-        arrived(out_q.at[source], o_recv.at[k - 1])
-    for q in range(n_tp):
-        out_ref[:, q * quarter:(q + 1) * quarter] = out_q[q]
-    for k in range(1, n_tp):
-        sent(part_in.at[k - 1], o_send.at[k - 1])
-
-
-def cache_kernel(pieces, pos, hidden_ref, k_new, v_new, k_hbm, v_hbm, out_ref, k_out, v_out, k_buf, v_buf, in_sem, out_sem):
+    out_ref[:, pl.ds(pl.multiple_of(tp * quarter, quarter), quarter)] = out_q[tp]
+    arrived(out_q.at[before, high], o_recv.at[2])
+    arrived(out_q.at[after, low], o_recv.at[3])
+    for place in (before, after):
+        out_ref[:, pl.ds(pl.multiple_of(place * quarter, quarter), quarter)] = out_q[place]
+    arrived(out_q.at[across, low], o_recv.at[4])
+    arrived(out_q.at[across, high], o_recv.at[5])
+    out_ref[:, pl.ds(pl.multiple_of(across * quarter, quarter), quarter)] = out_q[across]
+    for index in range(6):
+        sent(out_q.at[tp, low], o_send.at[index])
+
+
+def cache_kernel(pieces, pos, hidden, k_new_hbm, v_new_hbm, k_hbm, v_hbm, out, k_out, v_out, hidden_buf, k_new, v_new, k_buf, v_buf, in_sem, out_sem, sem):
     size = k_buf.shape[0] // pieces
     both = ((k_hbm, k_buf, k_out, k_new), (v_hbm, v_buf, v_out, v_new))
+    first = [
+        pltpu.make_async_copy(k_new_hbm, k_new, sem.at[0]),
+        pltpu.make_async_copy(v_new_hbm, v_new, sem.at[1]),
+    ]
+    hidden_in, hidden_out = (
+        pltpu.make_async_copy(hidden, hidden_buf, sem.at[2]), pltpu.make_async_copy(hidden_buf, out, sem.at[3]))
     loads = [
         [pltpu.make_async_copy(src.at[pl.ds(i * size, size)], buf.at[pl.ds(i * size, size)], in_sem.at[n, i])
          for n, (src, buf, _, _) in enumerate(both)] for i in range(pieces)]
     stores = [
         [pltpu.make_async_copy(buf.at[pl.ds(i * size, size)], dst.at[pl.ds(i * size, size)], out_sem.at[n, i])
          for n, (_, buf, dst, _) in enumerate(both)] for i in range(pieces)]
+    for load in first:
+        load.start()
     for pair in loads:
         for load in pair:
             load.start()
-    out_ref[...] = hidden_ref[...]
+    hidden_in.start()
+    for load in first:
+        load.wait()
     for i in range(pieces):
         for n, (_, buf, _, new) in enumerate(both):
             loads[i][n].wait()
             for t in range(i * size, (i + 1) * size):
                 buf[t, pos[t]] = new[t]
             stores[i][n].start()
+    hidden_in.wait()
+    hidden_out.start()
     for pair in stores:
         for store in pair:
             store.wait()
+    hidden_out.wait()
 
 
 def rope_table(cache_len, head_dim):
@@ -602,7 +640,7 @@
                 *[dma((n_tp - 1,))] * 4,
                 dma((n_tp,)), dma((n_tp,)),
                 dma((n_tp, 2)), dma((n_tp, 2)), dma((n_tp, 4)), dma((n_tp, 4)),
-                *[dma((n_tp - 1,))] * 4,
+                *[dma((n_tp - 1,))] * 2, dma((6,)), dma((6,)),
             ],
             compiler_params=pltpu.CompilerParams(
                 collective_id=0, has_side_effects=True, vmem_limit_bytes=67043328),
@@ -622,11 +660,13 @@
                 jax.ShapeDtypeStruct(k_cache.shape, BF16),
                 jax.ShapeDtypeStruct(v_cache.shape, BF16),
             ),
-            in_specs=[pl.BlockSpec(memory_space=pltpu.SMEM), vmem, vmem, vmem, hbm, hbm],
-            out_specs=(vmem, hbm, hbm),
+            in_specs=[pl.BlockSpec(memory_space=pltpu.SMEM)] + [hbm] * 5,
+            out_specs=(hbm, hbm, hbm),
             scratch_shapes=[
+                pltpu.VMEM(hidden_in.shape, BF16),
+                pltpu.VMEM((tokens, heads, head_dim), BF16), pltpu.VMEM((tokens, heads, head_dim), BF16),
                 pltpu.VMEM(k_cache.shape, BF16), pltpu.VMEM(v_cache.shape, BF16),
-                dma((2, 8)), dma((2, 8)),
+                dma((2, 8)), dma((2, 8)), dma((4,)),
             ],
         )(positions, hidden, k_new.reshape(tokens, heads, head_dim), v_new.reshape(tokens, heads, head_dim), k_cache, v_cache)
 

time: 88.4 us -> 84.9 us (0.960)
  Pallas kernels: 87.5 us -> 83.5 us
    pallas_call x1, Pallas kernels: 81.7 us -> 78.3 us  [local_layer(): pl.pallas_call(functools.partial(layer_kernel, n_tp, n_ep, 'ep', 'tp'), o...]
where the time goes in v3:
time: 84.9 us; the launch traced here: 84.3 us
  Pallas kernels  83.5 us (98%)
    pallas_call x1, Pallas kernels, local_layer(): pl.pallas_call(functools.partial(layer_kernel, n_tp, n_ep, 'ep', 'tp'), o...  78.3 us
    pallas_call x1, Pallas kernels, local_layer(): pl.pallas_call(functools.partial(cache_kernel, 8), out_shape=(jax.ShapeDt...  5.21 us

profile of v3, /device:TPU:96, one launch (start us, length us, event | category | flops | bytes accessed | tf_op | source)
XLA Modules:
  0.0 84.3 jit_solution(17683988551598849758)
XLA Ops:
  0.6 78.3 %shard_map.211 = (bf16[128,2048]{1,0:T(8,128)(2,1)}, bf16[512,128]{1,0:T(8,128)(2,1)}, bf16[512,128]{1,0:T(8,128)(2,1)}) custom-call(bf16[128,2048]{1,0:T(8,128)(2,1)} %x_ref.1, s32[1,128]{1,0:T(1,128)} %bitcast.32, s32[2,128]{1,0:T(2,128)} %bitcast.33, bf16[16,128]{1,0:T(8,128)(2,1)} %bitcast.29, bf16[16,128]{1,0:T(8,128)(2,1)} %bitcast.30, ...), custom_call_target="tpu_custom_call" | custom-call | tf_op jit(solution)/shard_map/pallas_call | solution.py:610
  79.0 5.2 %shard_map.212 = (bf16[128,2048]{1,0:T(8,128)(2,1)}, bf16[128,16,4,128]{3,2,1,0:T(4,128)(2,1)}, bf16[128,16,4,128]{3,2,1,0:T(4,128)(2,1)}) custom-call(s32[128]{0:T(128)} %pos.1, bf16[128,2048]{1,0:T(8,128)(2,1)} %get-tuple-element.6.hidden, bf16[128,4,128]{2,1,0:T(4,128)(2,1)} %bitcast.27, bf16[128,4,128]{2,1,0:T(4,128)(2,1)} %bitcast.28, ...), custom_call_target="tpu_custom_call" | custom-call | tf_op jit(solution)/shard_map/pallas_call | solution.py:656

commit v4 on v3

--- a/solution.py
+++ b/solution.py
@@ -61,7 +61,7 @@
     out_ref, k_new, v_new,
     eg, eu, ed, rows_all, meta, all_ids, part_q, part_in, h_q, c_buf, d_in, r1_in, r2_in, dense_q, fin_q, fin_in, out_q,
     sched_v, sched,
-    w_sem, e_sem, ag_send, ag_recv, m_send, m_recv, i_send, i_recv, a_send, a_recv, h_send, h_recv, d_send, d_recv,
+    w_sem, e_sem, ag_send, ag_recv, m_send, m_recv, i_send, i_recv, y_send, y_recv, a_send, a_recv, h_send, h_recv, d_send, d_recv,
     r1_send, r1_recv, r2_send, r2_recv, f_send, f_recv, o_send, o_recv,
 ):
     tokens, dim = x_ref.shape
@@ -110,18 +110,33 @@
 
     low, high = pl.ds(0, half), pl.ds(half, half)
 
-    def forward(index, place, rows):
+    messages = {1: (left, low), 2: (left, high), 3: (right, high), 4: (right, low), 5: (far, low), 6: (far, high)}
+    side = pl.ds(pl.multiple_of((tp % 2) * (dim // 2), dim // 2), dim // 2)
+    side_in = pl.ds(pl.multiple_of((1 - tp % 2) * (dim // 2), dim // 2), dim // 2)
+
+    def along_x(index):
+        place = {5: left, 6: right}.get(index, chip)
+        rows = messages[index][1]
+        block = rows_all.at[core, place, rows, side]
+        device = on_ring(right if index in (1, 2, 5) else left)
+        remote(block, block, ag_send.at[index], ag_recv.at[index], device).start()
+
+    def along_y(index):
+        place, rows = messages[index]
+        block = rows_all.at[core, place, rows, side]
+        arrived(block, ag_recv.at[index])
+        device = tp_peer(1) if rows is low else tp_peer(n_tp - 1)
+        remote(block, block, y_send.at[index - 1], y_recv.at[index - 1], device).start()
+
+    def across(index):
+        place, rows = messages[index]
+        arrived(rows_all.at[core, place, rows, side_in], y_recv.at[index - 1])
         block = rows_all.at[core, place, rows]
-        arrived(block, ag_recv.at[index])
         remote(block, block, ag_send.at[index + 6], ag_recv.at[index + 6], partner).start()
 
-    def forward_first():
-        forward(1, left, low)
-        block = rows_all.at[core, left, low]
-        remote(block, block, ag_send.at[5], ag_recv.at[5], on_ring(right)).start()
-        forward(3, right, high)
-        block = rows_all.at[core, right, high]
-        remote(block, block, ag_send.at[6], ag_recv.at[6], on_ring(left)).start()
+    def arrived_across(index):
+        place, rows = messages[index]
+        arrived(rows_all.at[other, place, rows], ag_recv.at[index + 6])
 
     barrier = pltpu.get_barrier_semaphore()
     for k in range(1, n_ep):
@@ -135,40 +150,41 @@
             for i, (src, dst) in enumerate(
                 ((wq_hbm, wq), (wk_hbm, wk), (wv_hbm, wv), (k_hbm, kc), (v_hbm, vc), (wo_hbm, wo)))
         ]
-        for load in loads:
-            load.start()
+        loads[0].start()
+
+        ids = ids_ref[...]
+        all_ids[core * n_x + chip] = jnp.concatenate([ids, jnp.zeros((6, tokens), jnp.int32)], axis=0)
+        pl.semaphore_wait(barrier, n_ep - 1 + n_tp - 1)
+        for k in range(1, n_ep):
+            block = all_ids.at[core * n_x + chip]
+            remote(block, block, i_send.at[k - 1], i_recv.at[k - 1], ep_peer(k)).start()
+
+        loads[1].start()
+        loads[2].start()
 
         moe_in = rms_norm(x_ref[...], as_row(n_post_ref[...]))
         rows_all[core, chip] = moe_in
+        along_x(1)
+        along_x(3)
+        own = rows_all.at[core, chip]
+        remote(own, own, ag_send.at[0], ag_recv.at[0], partner).start()
         logits = dot_nt(w_router_ref[...], moe_in)
         shifted = jnp.exp(logits - jnp.max(logits, axis=0, keepdims=True))
         probs = shifted / jnp.sum(shifted, axis=0, keepdims=True)
         expert_row = lax.broadcasted_iota(jnp.int32, probs.shape, 0)
-        ids = ids_ref[...]
         picked = [
             jnp.sum(jnp.where(expert_row == ids[k:k + 1, :], probs, 0.0), axis=0, keepdims=True) for k in range(2)
         ]
         total = picked[0] + picked[1]
         meta[core * n_x + chip] = jnp.concatenate(
             [picked[0] / total, picked[1] / total, jnp.zeros((6, tokens), F32)], axis=0)
-        all_ids[core * n_x + chip] = jnp.concatenate([ids, jnp.zeros((6, tokens), jnp.int32)], axis=0)
-
-        pl.semaphore_wait(barrier, n_ep - 1 + n_tp - 1)
-        own = rows_all.at[core, chip]
-        sends = [
-            remote(own.at[low], own.at[low], ag_send.at[1], ag_recv.at[1], on_ring(right)),
-            remote(own.at[high], own.at[high], ag_send.at[3], ag_recv.at[3], on_ring(left)),
-            remote(own.at[high], own.at[high], ag_send.at[2], ag_recv.at[2], on_ring(right)),
-            remote(own.at[low], own.at[low], ag_send.at[4], ag_recv.at[4], on_ring(left)),
-            remote(own, own, ag_send.at[0], ag_recv.at[0], partner),
-        ]
-        for k in range(1, n_ep):
-            block = meta.at[core * n_x + chip]
-            sends.append(remote(block, block, m_send.at[k - 1], m_recv.at[k - 1], ep_peer(k)))
-            block = all_ids.at[core * n_x + chip]
-            sends.append(remote(block, block, i_send.at[k - 1], i_recv.at[k - 1], ep_peer(k)))
-        for send in sends:
-            send.start()
+
+        def second_sends():
+            along_x(2)
+            along_x(4)
+            for k in range(1, n_ep):
+                block = meta.at[core * n_x + chip]
+                remote(block, block, m_send.at[k - 1], m_recv.at[k - 1], ep_peer(k)).start()
 
         normed = rms_norm(x_ref[...], as_row(n_in_ref[...]))
         pos_col = jnp.transpose(jnp.broadcast_to(pos_row_ref[...].astype(F32), (tokens, tokens)))
@@ -191,6 +207,10 @@
                 if dest is not v_s:
                     values = rotated(values)
                 dest[pl.ds(head, tokens, stride=heads), :] = values.astype(BF16).astype(F32)
+            if dest is q_s:
+                second_sends()
+                for later in loads[3:]:
+                    later.start()
         k_new[...] = k_s[...].astype(BF16)
         v_new[...] = v_s[...].astype(BF16)
 
@@ -232,18 +252,20 @@
                 o_s[r, :] = m
             return carry
 
-        lax.fori_loop(0, tokens // group // batch, attend, 0)
-
-        forward_first()
+        n_batches = tokens // group // batch
+        lax.fori_loop(0, n_batches // 2, attend, 0)
+        for index, onward in ((1, 5), (3, 6)):
+            along_y(index)
+            along_x(onward)
+        lax.fori_loop(n_batches // 2, n_batches, attend, 0)
 
         mixed = jnp.concatenate(
             [o_s[pl.ds(head, tokens, stride=heads), :] for head in range(heads)], axis=1).astype(BF16)
         loads[5].wait()
         for q in range(n_tp):
             part_q[q] = dot_nn(mixed, wo[:, q * quarter:(q + 1) * quarter]).astype(BF16)
-        for k in range(1, n_tp):
-            send = remote(part_q.at[(tp + k) % n_tp], part_in.at[k - 1], a_send.at[k - 1], a_recv.at[k - 1], tp_peer(k))
-            send.start()
+        along_y(2)
+        along_y(4)
 
     pl.run_scoped(
         attention_phase,
@@ -264,25 +286,23 @@
         for k in range(1, n_tp):
             remote(h_q.at[tp], h_q.at[tp], h_send.at[k - 1], h_recv.at[k - 1], tp_peer(k)).start()
 
-    def expert_phase(xs, sort, unsort, z, ys, y_sorted, weight_sorted, place_s, weight_s, act_s):
+    def expert_phase(xs, sort, unsort, z, ys, y_sorted, weight_sorted, place_s, act_s):
         for k in range(1, n_ep):
             source = (ep + n_ep - k) % n_ep
-            arrived(meta.at[(source % 2) * n_x + source // 2], m_recv.at[k - 1])
             arrived(all_ids.at[(source % 2) * n_x + source // 2], i_recv.at[k - 1])
         ids = [all_ids[:, k, :] for k in range(2)]
-        wts = [meta[:, k, :] for k in range(2)]
         first = ep * n_local
         lane = lax.broadcasted_iota(jnp.int32, (n_blocks, tokens), 1)
         start = jnp.zeros((n_blocks, tokens), jnp.int32)
         place = jnp.full((n_blocks, tokens), -1, jnp.int32)
-        weight = jnp.zeros((n_blocks, tokens), F32)
+        choice = jnp.zeros((n_blocks, tokens), jnp.int32)
         step_expert = jnp.zeros((n_blocks, tokens), jnp.int32)
         step_row = jnp.zeros((n_blocks, tokens), jnp.int32)
         block_row = jnp.zeros((n_blocks, tokens), jnp.int32)
         for e in range(n_local):
             here = [i == first + e for i in ids]
             hit = jnp.where(jnp.logical_or(here[0], here[1]), 1, 0)
-            weight = jnp.where(here[0], wts[0], jnp.where(here[1], wts[1], weight))
+            choice = jnp.where(here[1], 1, choice)
             scan = lane_scan(hit)
             totals = jnp.broadcast_to(scan[:, tokens - 1:], scan.shape)
             above = row_scan(totals)
@@ -308,57 +328,68 @@
         to_scalar.start()
 
         place_s[...] = place
-        weight_s[...] = weight
         row_id = lax.broadcasted_iota(jnp.int32, (n_sorted, tokens), 0)
-        weight_rows = jnp.zeros((n_sorted, tokens), F32)
-        spots = (chip, left, right, far)
-        for n, spot in enumerate(spots):
-            for c in range(2):
-                source = pl.ds(c * n_x + spot, 1)
-                match = row_id == place_s[source, :]
-                first_col = (2 * n + c) * tokens
+        groups = (
+            ((core, chip), (other, chip)), ((core, left), (core, right)), ((other, left), (other, right)),
+            ((core, far), (other, far)))
+        for n, pair in enumerate(groups):
+            for m, (c, spot) in enumerate(pair):
+                match = row_id == place_s[pl.ds(c * n_x + spot, 1), :]
+                first_col = (2 * n + m) * tokens
                 sort[:, first_col:first_col + tokens] = jnp.where(match, 1.0, 0.0).astype(BF16)
-                weight_rows = weight_rows + jnp.where(match, weight_s[source, :], 0.0)
-        weight_sorted[0:n_sorted, :] = jnp.broadcast_to(
-            jnp.sum(weight_rows, axis=1, keepdims=True), (n_sorted, 128))
-        weight_sorted[n_sorted:, :] = jnp.zeros((ROWS, 128), F32)
+
+        def sort_weights():
+            for k in range(1, n_ep):
+                source = (ep + n_ep - k) % n_ep
+                arrived(meta.at[(source % 2) * n_x + source // 2], m_recv.at[k - 1])
+            weight = jnp.where(choice == 1, meta[:, 1, :], meta[:, 0, :])
+            weight_rows = jnp.zeros((n_sorted, tokens), F32)
+            for j in range(n_blocks):
+                weight_rows = weight_rows + jnp.where(row_id == place[j:j + 1, :], weight[j:j + 1, :], 0.0)
+            weight_sorted[0:n_sorted, :] = jnp.broadcast_to(
+                jnp.sum(weight_rows, axis=1, keepdims=True), (n_sorted, 128))
+            weight_sorted[n_sorted:, :] = jnp.zeros((ROWS, 128), F32)
+
         xs[n_sorted:, :] = jnp.zeros((ROWS, dim), BF16)
+        def add_rows(n):
+            def one(i, carry):
+                cols = pl.ds(pl.multiple_of(i * 256, 256), 256)
+                rows = jnp.concatenate([rows_all[c, spot, :, cols] for c, spot in groups[n]], axis=0)
+                total = dot_nn(sort[:, 2 * n * tokens:(2 * n + 2) * tokens], rows)
+                if n > 0:
+                    total = total + xs[0:n_sorted, cols].astype(F32)
+                xs[0:n_sorted, cols] = total.astype(BF16)
+                return carry
+
+            lax.fori_loop(0, dim // 256, one, 0, unroll=2)
+
+        arrived(rows_all.at[other, chip], ag_recv.at[0])
+        add_rows(0)
+        along_y(5)
+        along_y(6)
+        for index in (1, 3, 2, 4):
+            across(index)
+        add_rows(1)
+        for index in (5, 6):
+            across(index)
+        for k in range(1, n_tp):
+            remote(part_q.at[(tp + k) % n_tp], part_in.at[k - 1], a_send.at[k - 1], a_recv.at[k - 1], tp_peer(k)).start()
         place_cols = jnp.transpose(place.astype(F32))
         column_id = lax.broadcasted_iota(jnp.int32, (tokens, n_sorted), 1).astype(F32)
         for j in range(n_blocks):
             unsort[j * tokens:(j + 1) * tokens, :] = jnp.where(
                 column_id == place_cols[:, j:j + 1], 1.0, 0.0).astype(BF16)
-
-        forward(2, left, high)
-        forward(4, right, low)
-        attention_sum()
-
-        def add_rows(numbers):
-            def one(i, carry):
-                cols = pl.ds(pl.multiple_of(i * 256, 256), 256)
-                total = None
-                for n in numbers:
-                    rows = rows_all[:, spots[n], :, cols].reshape(2 * tokens, 256)
-                    part = dot_nn(sort[:, 2 * n * tokens:(2 * n + 2) * tokens], rows)
-                    total = part if total is None else total + part
-                if numbers[0] > 0:
-                    total = total + xs[0:n_sorted, cols].astype(F32)
-                xs[0:n_sorted, cols] = total.astype(BF16)
-                return carry
-
-            lax.fori_loop(0, dim // 256, one, 0, unroll=2)
-
-        arrived(rows_all.at[other, chip], ag_recv.at[0])
-        for index, spot, part in ((1, left, low), (2, left, high), (3, right, high), (4, right, low)):
-            arrived(rows_all.at[other, spot, part], ag_recv.at[index + 6])
-        add_rows((0, 1, 2))
-        forward(5, far, low)
-        forward(6, far, high)
-        for index, part in ((5, low), (6, high)):
-            arrived(rows_all.at[other, far, part], ag_recv.at[index + 6])
-        add_rows((3,))
-        for index in range(1, 13):
-            sent(rows_all.at[core, chip, low], ag_send.at[index])
+        sort_weights()
+        for index in (1, 3, 2, 4):
+            arrived_across(index)
+        add_rows(2)
+        for index in (5, 6):
+            arrived_across(index)
+        add_rows(3)
+        for index in messages:
+            sent(rows_all.at[core, chip, low, side], ag_send.at[index])
+            sent(rows_all.at[core, chip, low, side], y_send.at[index - 1])
+            sent(rows_all.at[core, chip, low], ag_send.at[index + 6])
         sent(rows_all.at[core, chip], ag_send.at[0])
         for k in range(1, n_ep):
             sent(meta.at[core * n_x + chip], m_send.at[k - 1])
@@ -384,7 +415,7 @@
         for e in range(n_local):
             pltpu.make_async_copy(ed_hbm.at[e], ed.at[e], e_sem.at[2, e]).wait()
 
-        def compute(i):
+        def results(i):
             cols = columns(i)
 
             def down(step, carry):
@@ -402,27 +433,39 @@
                 return carry
 
             lax.fori_loop(0, n_sorted // ALIGN, regroup, 0, unroll=8)
+
+        def to_tokens(i):
+            cols = columns(i)
             for c in range(2):
                 back = dot_nn(unsort[c * n_x * tokens:(c + 1) * n_x * tokens, :], y_sorted[...])
                 rows_all[c, :, :, cols] = back.astype(BF16).reshape(n_x, tokens, quarter)
             remote(rows_all.at[other, :, :, cols], d_in.at[i], d_send.at[i], d_recv.at[i], partner).start()
 
-        compute(0)
+        attention_sum()
+        results(0)
+        to_tokens(0)
+        results(1)
+        pair_sum(0)
+        pair_sum_rest(0)
+        to_tokens(1)
+        results(2)
+        pair_sum(1)
+        pair_sum_rest(1)
+        to_tokens(2)
+        ring_sum(0)
+        results(3)
+        pair_sum(2)
+        pair_sum_rest(2)
+        to_tokens(3)
+        ring_sum(1)
+        pair_sum(3)
+        ring_sum(2)
         dense_gate_up(act_s)
-        pair_sum(0)
-        compute(1)
-        ring_sum(0)
+        pair_sum_rest(3)
         dense_down(act_s)
-        pair_sum(1)
-        compute(2)
-        ring_sum(1)
+        ring_sum(3)
         finish(0)
-        pair_sum(2)
-        compute(3)
-        ring_sum(2)
         finish(1)
-        pair_sum(3)
-        ring_sum(3)
         finish(2)
         finish(3)
 
@@ -437,6 +480,9 @@
                 rows_all[core, spot, :, cols].astype(F32) + d_in[i, spot].astype(F32)).astype(BF16)
         remote(rows_all.at[core, far, low, cols], r1_in.at[i, 0], r1_send.at[i, 0], r1_recv.at[i, 0], on_ring(right)).start()
         remote(rows_all.at[core, far, high, cols], r1_in.at[i, 1], r1_send.at[i, 1], r1_recv.at[i, 1], on_ring(left)).start()
+
+    def pair_sum_rest(i):
+        cols = columns(i)
         remote(rows_all.at[core, right, high, cols], r2_in.at[i, 0, high], r2_send.at[i, 0], r2_recv.at[i, 0], on_ring(right)).start()
         remote(rows_all.at[core, left, low, cols], r2_in.at[i, 1, low], r2_send.at[i, 1], r2_recv.at[i, 1], on_ring(left)).start()
 
@@ -500,10 +546,9 @@
         pltpu.VMEM((n_sorted, quarter), BF16),
         pltpu.VMEM((n_sorted + ROWS, 128), F32),
         pltpu.VMEM((n_blocks, tokens), jnp.int32),
-        pltpu.VMEM((n_blocks, tokens), F32),
         pltpu.VMEM((dense_parts, tokens, width), BF16),
     )
-    before, after, across = (tp + n_tp - 1) % n_tp, (tp + 1) % n_tp, (tp + 2) % n_tp
+    before, after, opposite = (tp + n_tp - 1) % n_tp, (tp + 1) % n_tp, (tp + 2) % n_tp
     up, down = tp_peer(1), tp_peer(n_tp - 1)
 
     def pass_on(index, place, rows, device):
@@ -512,6 +557,9 @@
 
     pass_on(0, tp, low, up)
     pass_on(1, tp, high, down)
+    out_ref[:, pl.ds(pl.multiple_of(tp * quarter, quarter), quarter)] = out_q[tp]
+    for index in range(2):
+        sent(out_q.at[tp, low], o_send.at[index])
     pass_on(2, tp, high, up)
     pass_on(3, tp, low, down)
     arrived(out_q.at[before, low], o_recv.at[0])
@@ -530,15 +578,14 @@
         sent(part_in.at[k - 1], a_send.at[k - 1])
         sent(part_in.at[k - 1], h_send.at[k - 1])
         sent(part_in.at[k - 1], f_send.at[k - 1])
-    out_ref[:, pl.ds(pl.multiple_of(tp * quarter, quarter), quarter)] = out_q[tp]
     arrived(out_q.at[before, high], o_recv.at[2])
     arrived(out_q.at[after, low], o_recv.at[3])
     for place in (before, after):
         out_ref[:, pl.ds(pl.multiple_of(place * quarter, quarter), quarter)] = out_q[place]
-    arrived(out_q.at[across, low], o_recv.at[4])
-    arrived(out_q.at[across, high], o_recv.at[5])
-    out_ref[:, pl.ds(pl.multiple_of(across * quarter, quarter), quarter)] = out_q[across]
-    for index in range(6):
+    arrived(out_q.at[opposite, low], o_recv.at[4])
+    arrived(out_q.at[opposite, high], o_recv.at[5])
+    out_ref[:, pl.ds(pl.multiple_of(opposite * quarter, quarter), quarter)] = out_q[opposite]
+    for index in range(2, 6):
         sent(out_q.at[tp, low], o_send.at[index])
 
 
@@ -636,7 +683,7 @@
                 pltpu.VMEM((n_tp, tokens, quarter), BF16),
                 pltpu.VMEM((n_ep, tokens), jnp.int32),
                 pltpu.SMEM((n_ep, tokens), jnp.int32),
-                dma((9,)), dma((3, n_local)), dma((13,)), dma((13,)), *[dma((n_ep - 1,))] * 4,
+                dma((9,)), dma((3, n_local)), dma((13,)), dma((13,)), *[dma((n_ep - 1,))] * 4, dma((6,)), dma((6,)),
                 *[dma((n_tp - 1,))] * 4,
                 dma((n_tp,)), dma((n_tp,)),
                 dma((n_tp, 2)), dma((n_tp, 2)), dma((n_tp, 4)), dma((n_tp, 4)),

time: 84.9 us -> 79.8 us (0.940)
  Pallas kernels: 83.5 us -> 78.9 us
    pallas_call x1, Pallas kernels: 78.3 us -> 73.7 us  [local_layer(): pl.pallas_call(functools.partial(layer_kernel, n_tp, n_ep, 'ep', 'tp'), o...]
where the time goes in v4:
time: 79.8 us; the launch traced here: 79.7 us
  Pallas kernels  78.9 us (99%)
  between operations  0.83 us (1%)
    pallas_call x1, Pallas kernels, local_layer(): pl.pallas_call(functools.partial(layer_kernel, n_tp, n_ep, 'ep', 'tp'), o...  73.7 us
    pallas_call x1, Pallas kernels, local_layer(): pl.pallas_call(functools.partial(cache_kernel, 8), out_shape=(jax.ShapeDt...  5.21 us

profile of v4, /device:TPU:96, one launch (start us, length us, event | category | flops | bytes accessed | tf_op | source)
XLA Modules:
  0.0 79.7 jit_solution(5354116257945726712)
XLA Ops:
  0.6 73.7 %shard_map.211 = (bf16[128,2048]{1,0:T(8,128)(2,1)}, bf16[512,128]{1,0:T(8,128)(2,1)}, bf16[512,128]{1,0:T(8,128)(2,1)}) custom-call(bf16[128,2048]{1,0:T(8,128)(2,1)} %x_ref.1, s32[1,128]{1,0:T(1,128)} %bitcast.32, s32[2,128]{1,0:T(2,128)} %bitcast.33, bf16[16,128]{1,0:T(8,128)(2,1)} %bitcast.29, bf16[16,128]{1,0:T(8,128)(2,1)} %bitcast.30, ...), custom_call_target="tpu_custom_call" | custom-call | tf_op jit(solution)/shard_map/pallas_call | solution.py:657
  74.3 5.2 %shard_map.212 = (bf16[128,2048]{1,0:T(8,128)(2,1)}, bf16[128,16,4,128]{3,2,1,0:T(4,128)(2,1)}, bf16[128,16,4,128]{3,2,1,0:T(4,128)(2,1)}) custom-call(s32[128]{0:T(128)} %pos.1, bf16[128,2048]{1,0:T(8,128)(2,1)} %get-tuple-element.6.hidden, bf16[128,4,128]{2,1,0:T(4,128)(2,1)} %bitcast.27, bf16[128,4,128]{2,1,0:T(4,128)(2,1)} %bitcast.28, ...), custom_call_target="tpu_custom_call" | custom-call | tf_op jit(solution)/shard_map/pallas_call | solution.py:703

commit v5 on v4

--- a/solution.py
+++ b/solution.py
@@ -152,18 +152,17 @@
         ]
         loads[0].start()
 
+        for later in loads[1:]:
+            later.start()
+
+        moe_in = rms_norm(x_ref[...], as_row(n_post_ref[...]))
+        rows_all[core, chip] = moe_in
         ids = ids_ref[...]
         all_ids[core * n_x + chip] = jnp.concatenate([ids, jnp.zeros((6, tokens), jnp.int32)], axis=0)
         pl.semaphore_wait(barrier, n_ep - 1 + n_tp - 1)
         for k in range(1, n_ep):
             block = all_ids.at[core * n_x + chip]
             remote(block, block, i_send.at[k - 1], i_recv.at[k - 1], ep_peer(k)).start()
-
-        loads[1].start()
-        loads[2].start()
-
-        moe_in = rms_norm(x_ref[...], as_row(n_post_ref[...]))
-        rows_all[core, chip] = moe_in
         along_x(1)
         along_x(3)
         own = rows_all.at[core, chip]
@@ -209,8 +208,6 @@
                 dest[pl.ds(head, tokens, stride=heads), :] = values.astype(BF16).astype(F32)
             if dest is q_s:
                 second_sends()
-                for later in loads[3:]:
-                    later.start()
         k_new[...] = k_s[...].astype(BF16)
         v_new[...] = v_s[...].astype(BF16)
 
@@ -252,12 +249,10 @@
                 o_s[r, :] = m
             return carry
 
-        n_batches = tokens // group // batch
-        lax.fori_loop(0, n_batches // 2, attend, 0)
+        lax.fori_loop(0, tokens // group // batch, attend, 0)
         for index, onward in ((1, 5), (3, 6)):
             along_y(index)
             along_x(onward)
-        lax.fori_loop(n_batches // 2, n_batches, attend, 0)
 
         mixed = jnp.concatenate(
             [o_s[pl.ds(head, tokens, stride=heads), :] for head in range(heads)], axis=1).astype(BF16)
@@ -426,7 +421,7 @@
                 ys[pl.ds(pl.multiple_of(step * ROWS, ROWS), ROWS), :] = jnp.concatenate(scaled, axis=1).astype(BF16)
                 return carry
 
-            lax.fori_loop(0, n_steps, down, 0, unroll=3)
+            lax.fori_loop(0, n_steps, down, 0, unroll=9)
 
             def regroup(b, carry):
                 y_sorted[pl.ds(pl.multiple_of(b * ALIGN, ALIGN), ALIGN), :] = ys[pl.ds(sched[2, b] * ALIGN, ALIGN), :]
@@ -436,9 +431,8 @@
 
         def to_tokens(i):
             cols = columns(i)
-            for c in range(2):
-                back = dot_nn(unsort[c * n_x * tokens:(c + 1) * n_x * tokens, :], y_sorted[...])
-                rows_all[c, :, :, cols] = back.astype(BF16).reshape(n_x, tokens, quarter)
+            back = dot_nn(unsort[...], y_sorted[...])
+            rows_all[:, :, :, cols] = back.astype(BF16).reshape(2, n_x, tokens, quarter)
             remote(rows_all.at[other, :, :, cols], d_in.at[i], d_send.at[i], d_recv.at[i], partner).start()
 
         attention_sum()

time: 79.8 us -> 79.5 us (level)
  no operation moved by 1% of the time
where the time goes in v5:
time: 79.5 us; the launch traced here: 79.4 us
  Pallas kernels  78.6 us (99%)
  between operations  0.83 us (1%)
    pallas_call x1, Pallas kernels, local_layer(): pl.pallas_call(functools.partial(layer_kernel, n_tp, n_ep, 'ep', 'tp'), o...  73.4 us
    pallas_call x1, Pallas kernels, local_layer(): pl.pallas_call(functools.partial(cache_kernel, 8), out_shape=(jax.ShapeDt...  5.21 us

profile of v5, /device:TPU:96, one launch (start us, length us, event | category | flops | bytes accessed | tf_op | source)
XLA Modules:
  0.0 79.4 jit_solution(16155642301015812082)
XLA Ops:
  0.6 73.4 %shard_map.211 = (bf16[128,2048]{1,0:T(8,128)(2,1)}, bf16[512,128]{1,0:T(8,128)(2,1)}, bf16[512,128]{1,0:T(8,128)(2,1)}) custom-call(bf16[128,2048]{1,0:T(8,128)(2,1)} %x_ref.1, s32[1,128]{1,0:T(1,128)} %bitcast.32, s32[2,128]{1,0:T(2,128)} %bitcast.33, bf16[16,128]{1,0:T(8,128)(2,1)} %bitcast.29, bf16[16,128]{1,0:T(8,128)(2,1)} %bitcast.30, ...), custom_call_target="tpu_custom_call" | custom-call | tf_op jit(solution)/shard_map/pallas_call | solution.py:651
  74.0 5.2 %shard_map.212 = (bf16[128,2048]{1,0:T(8,128)(2,1)}, bf16[128,16,4,128]{3,2,1,0:T(4,128)(2,1)}, bf16[128,16,4,128]{3,2,1,0:T(4,128)(2,1)}) custom-call(s32[128]{0:T(128)} %pos.1, bf16[128,2048]{1,0:T(8,128)(2,1)} %get-tuple-element.6.hidden, bf16[128,4,128]{2,1,0:T(4,128)(2,1)} %bitcast.27, bf16[128,4,128]{2,1,0:T(4,128)(2,1)} %bitcast.28, ...), custom_call_target="tpu_custom_call" | custom-call | tf_op jit(solution)/shard_map/pallas_call | solution.py:697
